TPU v7x, 128 devices: a whole 4x4x4 slice. The times are simulated.
128 devices in a mesh: dom: 16 (over y, z), sub: 8 (over x, core).
Axes of the slice: x: 4, y: 4, z: 4, core: 2. Of those that a mesh axis runs over, the one named last changes fastest.
Arguments:
- positions: float32 [3, 524288], P(None, ('dom', 'sub')), may hold values from -20 to 20
- mass: float32 [524288], P(('dom', 'sub')), may hold values from 3 to 6
- local_tiles: float32 [8192, 128, 128], P(('dom', 'sub')), as said below
- local_rows: int32 [8192], P(('dom', 'sub')), may hold values from 0 to 31, as said below
- local_cols: int32 [8192], P(('dom', 'sub')), may hold values from 0 to 31, as said below
- live_tiles: int32 [128], P(('dom', 'sub')), may hold values from 32 to 64, as said below
- dom_tiles: float32 [4096, 128, 128], P(('dom', 'sub')), as said below
- dom_cols: int32 [4096], P(('dom', 'sub')), may hold values from 0 to 31
- dom_slots: int32 [4096], P(('dom', 'sub')), may hold values from 0 to 511, as said below
- dom_rows: int32 [65536], P(('dom', 'sub')), may hold values from 0 to 31, as said below
- sub_tiles: float32 [6144, 128, 128], P(('dom', 'sub')), as said below
- sub_cols: int32 [6144], P(('dom', 'sub')), may hold values from 0 to 31
- sub_slots: int32 [6144], P(('dom', 'sub')), may hold values from 0 to 63, as said below
- sub_rows: int32 [8192], P(('dom', 'sub')), may hold values from 0 to 31, as said below
- precond: float32 [4096, 128, 128], P(('dom', 'sub')), may hold values from -0.05 to 0.3, as said below
Outputs:
- solution: float32 [3, 524288], P(None, ('dom', 'sub'))
- residual: float32 [3, 524288], P(None, ('dom', 'sub'))
Inputs may be any that keep to these rules, and one draw needn't show every extreme that they name: Device d uses the first live_tiles[d] of its 64 interior tiles, an even number; some device uses all of them. `local_tiles`: interior tiles come in pairs 2i, 2i + 1 of a device: the second is the transpose of the first. `local_rows`: tile 2i + 1 of a device has the block row and column of tile 2i swapped. `local_cols`: tile 2i + 1 of a device has the block row and column of tile 2i swapped. `dom_slots`: the destination group of a tile differs from its device's dom index in exactly one of its 4 bits; no two tiles of a device share a slot. `dom_rows`: entries for slots that no tile fills are arbitrary blocks of the receiver. `dom_tiles`: every coupling tile that reaches block row r of a device from block column c of another has a transposed tile on the receiver, from its block column r, that reaches block row c of the sender; so A is symmetric. `sub_slots`: the destination partition of a tile lies in its device's group and is not its device's own; no two tiles of a device share a slot. `sub_rows`: entries for slots that no tile fills are arbitrary blocks of the receiver. `sub_tiles`: every such tile has a transposed partner on the receiving partition that is routed back to the sender's block column. `precond`: every block is symmetric and positive definite.
All inputs are finite; a program needn't handle non-finite values.
Results may differ from a plain program's by a relative error of at most 0.0003.
Values sent between devices are 32-bit elements; how exact they have to be, the bound alone decides.
A program may use at most 64 MiB of HBM per device.

v0:
```python
import functools

import jax
import jax.numpy as jnp
from jax import lax
from jax.experimental import pallas as pl
from jax.experimental.pallas import tpu as pltpu
from jax.sharding import PartitionSpec as P

TILE = 128
DIMS = 3
NB = 32
LT = 64
IFD = 32
IFS = 48
SD = 32
SS = 8
N_DOM = 16
N_SUB = 8
BITS = 4
PHASES = 4
SHIFT = 0.9

PAIR_L = 0
PAIR_S = LT // 2
PAIR_D = PAIR_S + IFS // 2
PAIR_P = PAIR_D + IFD // 2
PAIRS = PAIR_P + NB // 2
GROUP = 16

BASE_D = NB
BASE_S = NB + BITS * NB
ROWS_X = BASE_S + N_SUB * SS

F32 = jnp.float32
BF16 = jnp.bfloat16


def kernel(
    pos_h,
    mass_h,
    lt_h,
    lrow_h,
    lcol_h,
    live_h,
    dt_h,
    dcol_h,
    dslot_h,
    drow_h,
    st_h,
    scol_h,
    sslot_h,
    srow_h,
    pt_h,
    sol_o,
    res_o,
    x_v,
    x3,
    q_v,
    w_v,
    mass_v,
    land,
    tb,
    xg,
    prod,
    acc,
    got_d,
    got_s,
    pack,
    sel_l,
    sel_s,
    sel_d,
    lcol_v,
    scol_v,
    dcol_v,
    drow_v,
    drow_r,
    part,
    row1,
    got1,
    row2,
    got2,
    lrow_m,
    live_m,
    sslot_m,
    srow_m,
    dslot_m,
    drow_m,
    idx,
    in_sem,
    tile_sem,
    ix_send,
    ix_recv,
    ix_loc,
    sd_send,
    sd_recv,
    ss_send,
    ss_recv,
    a1_send,
    a1_recv,
    a2_send,
    a2_recv,
):
    a = lax.axis_index("dom")
    b = lax.axis_index("sub")

    def dom_dev(j):
        return {"dom": jnp.bitwise_xor(a, 1 << j)}

    def sub_dev(o):
        return {"sub": lax.rem(b + o, N_SUB)}

    small = [
        (pos_h, x_v.at[0]),
        (drow_h, drow_v),
        (mass_h, mass_v),
        (lrow_h, lrow_m),
        (live_h, live_m),
        (sslot_h, sslot_m),
        (srow_h, srow_m),
        (dslot_h, dslot_m),
        (lcol_h, lcol_v),
        (scol_h, scol_v),
        (dcol_h, dcol_v),
    ]
    small = [
        pltpu.make_async_copy(src, dst, in_sem.at[i]) for i, (src, dst) in enumerate(small)
    ]
    for copy in small:
        copy.start()
    loads = []
    for src, first in ((lt_h, PAIR_L), (st_h, PAIR_S), (dt_h, PAIR_D), (pt_h, PAIR_P)):
        for start in range(0, src.shape[0], GROUP):
            loads.append(
                pltpu.make_async_copy(
                    src.at[pl.ds(start, GROUP)],
                    land.at[pl.ds(2 * first + start, GROUP)],
                    tile_sem.at[len(loads)],
                )
            )
    for copy in loads:
        copy.start()

    barrier = pltpu.get_barrier_semaphore()
    for j in range(BITS):
        pl.semaphore_signal(barrier, inc=1, device_id=dom_dev(j))
    for o in range(1, N_SUB):
        pl.semaphore_signal(barrier, inc=1, device_id=sub_dev(o))
    pl.semaphore_wait(barrier, BITS + N_SUB - 1)

    def dom_copy(p, j):
        return pltpu.make_async_remote_copy(
            src_ref=x_v.at[p],
            dst_ref=got_d.at[p, j],
            send_sem=sd_send.at[p, j],
            recv_sem=sd_recv.at[p, j],
            device_id=dom_dev(j),
        )

    def sub_copy(p, o):
        return pltpu.make_async_remote_copy(
            src_ref=pack.at[p, o - 1],
            dst_ref=got_s.at[p, N_SUB - 1 - o],
            send_sem=ss_send.at[p, o - 1],
            recv_sem=ss_recv.at[p, N_SUB - 1 - o],
            device_id=sub_dev(o),
        )

    def sub_arrival(p, e):
        return pltpu.make_async_remote_copy(
            src_ref=pack.at[p, e],
            dst_ref=got_s.at[p, e],
            send_sem=ss_send.at[p, e],
            recv_sem=ss_recv.at[p, e],
            device_id=sub_dev(e + 1),
        )

    def row_copy(j):
        return pltpu.make_async_remote_copy(
            src_ref=drow_v,
            dst_ref=drow_r.at[j],
            send_sem=ix_send.at[j],
            recv_sem=ix_recv.at[j],
            device_id=dom_dev(j),
        )

    def send(p):
        for j in range(BITS):
            dom_copy(p, j).start()

        def gather(i, carry):
            for s in range(SS):
                block = srow_m[lax.rem(b + i + 1, N_SUB) * SS + s]
                rows = x3[p, block]
                for k in range(DIMS):
                    pack[p, i, k, pl.ds(s, 1), :] = rows[k : k + 1]
            return carry

        for k in range(DIMS):
            x3[p, :, k, :] = x_v[p, k]
        lax.fori_loop(0, N_SUB - 1, gather, 0)
        for o in range(1, N_SUB):
            sub_copy(p, o).start()

    xg3 = xg.reshape(ROWS_X, 8, TILE)

    def split(base, count, values):
        for k in range(DIMS):
            high = values[k].astype(BF16).astype(F32)
            xg[pl.ds(base * 8 + k, count, stride=8), :] = high
            xg[pl.ds(base * 8 + DIMS + k, count, stride=8), :] = values[k] - high

    def multiply(pair, first, second, slot):
        left = jnp.concatenate(
            [xg3[first], xg3[second]],
            axis=0,
        ).astype(BF16)
        out = jnp.dot(
            jnp.concatenate([left, left], axis=1), tb[pair], preferred_element_type=F32
        )
        prod[pl.ds(pl.multiple_of(slot * 16, 16), 8), :] = out[0:8, 0:TILE]
        prod[pl.ds(pl.multiple_of(slot * 16 + 8, 8), 8), :] = out[8:16, TILE : 2 * TILE]

    def run(first, count):
        def body(i, carry):
            pair = first + i
            multiply(pair, idx[2 * pair], idx[2 * pair + 1], pair)
            return carry

        lax.fori_loop(0, count, body, 0, unroll=8)

    def taken(first, count, k):
        return (
            prod[pl.ds(first * 16 + k, count, stride=8), :]
            + prod[pl.ds(first * 16 + DIMS + k, count, stride=8), :]
        )

    def combine(select, first, count):
        terms = []
        for k in range(DIMS):
            value = taken(first, count, k)
            high = value.astype(BF16)
            rest = value - high.astype(F32)
            middle = rest.astype(BF16)
            terms += [high, middle, (rest - middle.astype(F32)).astype(BF16)]
        out = jnp.dot(
            select[...], jnp.concatenate(terms, axis=1), preferred_element_type=F32
        )
        sums = []
        for k in range(DIMS):
            at = 3 * k * TILE
            sums.append(
                out[:, at + 2 * TILE : at + 3 * TILE]
                + out[:, at + TILE : at + 2 * TILE]
                + out[:, at : at + TILE]
            )
        return sums

    small[0].wait()
    small[1].wait()
    for j in range(BITS):
        row_copy(j).start()
    for copy in small[2:]:
        copy.wait()
    send(0)

    block_ids = lax.broadcasted_iota(jnp.int32, (NB, LT), 0)
    tile_ids = lax.broadcasted_iota(jnp.int32, (NB, LT), 1)
    hit = jnp.logical_and(lcol_v[...] == block_ids, tile_ids < live_m[0])
    sel_l[...] = jnp.where(hit, 1.0, 0.0).astype(BF16)
    sel_s[...] = jnp.where(
        scol_v[...] == lax.broadcasted_iota(jnp.int32, (NB, IFS), 0), 1.0, 0.0
    ).astype(BF16)
    sel_d[...] = jnp.where(
        dcol_v[...] == lax.broadcasted_iota(jnp.int32, (NB, IFD), 0), 1.0, 0.0
    ).astype(BF16)
    xg[...] = jnp.zeros_like(xg)

    def put_local(t, carry):
        idx[t] = lrow_m[t]
        return carry

    def put_sub(t, carry):
        slot = sslot_m[t]
        place = jnp.bitwise_and(jnp.right_shift(slot, 3) - b - 1, N_SUB - 1)
        idx[2 * PAIR_S + t] = BASE_S + place * SS + jnp.bitwise_and(slot, SS - 1)
        return carry

    lax.fori_loop(0, LT, put_local, 0, unroll=8)
    lax.fori_loop(0, IFS, put_sub, 0, unroll=8)

    def convert(i, carry):
        for half in range(2):
            tile = land[2 * i + half]
            high = tile.astype(BF16)
            low = (tile - high.astype(F32)).astype(BF16)
            tb[i, 0:TILE, half * TILE : (half + 1) * TILE] = high
            tb[i, TILE : 2 * TILE, half * TILE : (half + 1) * TILE] = low
        return carry

    for n, copy in enumerate(loads):
        copy.wait()
        lax.fori_loop(n * GROUP // 2, (n + 1) * GROUP // 2, convert, 0)

    for j in range(BITS):
        row_copy(j).wait_recv()
    moved = pltpu.make_async_copy(drow_r, drow_m, ix_loc)
    moved.start()
    moved.wait()

    def put_dom(t, carry):
        slot = dslot_m[t]
        other = jnp.bitwise_xor(jnp.right_shift(slot, 5), a)
        bit = (
            (other >= 2).astype(jnp.int32)
            + (other >= 4).astype(jnp.int32)
            + (other >= 8).astype(jnp.int32)
        )
        place = a * SD + jnp.bitwise_and(slot, SD - 1)
        block = drow_m[bit, jnp.right_shift(place, 7), jnp.bitwise_and(place, TILE - 1)]
        idx[2 * PAIR_D + t] = BASE_D + bit * NB + block
        return carry

    lax.fori_loop(0, IFD, put_dom, 0, unroll=8)

    def phase(p, carry):
        @pl.when(p > 0)
        def _():
            send(p)

        split(0, NB, [x_v[p, k] for k in range(DIMS)])
        run(PAIR_L, LT // 2)
        for e in range(N_SUB - 1):
            sub_arrival(p, e).wait_recv()
            split(BASE_S + e * SS, SS, [got_s[p, e, k] for k in range(DIMS)])
        run(PAIR_S, IFS // 2)
        inner = combine(sel_l, PAIR_L, LT)
        middle = combine(sel_s, PAIR_S, IFS)
        for k in range(DIMS):
            acc[k] = mass_v[...] * x_v[p, k] + (inner[k] + middle[k])
        for j in range(BITS):
            dom_copy(p, j).wait_recv()
            split(BASE_D + j * NB, NB, [got_d[p, j, k] for k in range(DIMS)])
        run(PAIR_D, IFD // 2)
        outer = combine(sel_d, PAIR_D, IFD)

        @pl.when(p == 0)
        def _():
            for k in range(DIMS):
                q_v[0, k] = mass_v[...] * x_v[0, k] - (acc[k] + outer[k])

        @pl.when(p > 0)
        def _():
            for k in range(DIMS):
                w_v[p - 1, k] = acc[k] + outer[k]

        @pl.when(jnp.logical_and(p > 0, p < PHASES - 1))
        def _():
            for k in range(DIMS):
                q_v[p, k] = w_v[p - 1, k] - SHIFT * q_v[p - 1, k]

        @pl.when(p < PHASES - 1)
        def _():
            split(0, NB, [q_v[p, k] for k in range(DIMS)])

            def body(i, carry):
                multiply(PAIR_P + i, 2 * i, 2 * i + 1, PAIR_P + i)
                return carry

            lax.fori_loop(0, NB // 2, body, 0, unroll=8)
            for k in range(DIMS):
                x_v[p + 1, k] = taken(PAIR_P, NB, k)

        for j in range(BITS):
            dom_copy(p, j).wait_send()
        for o in range(1, N_SUB):
            sub_copy(p, o).wait_send()
        return carry

    lax.fori_loop(0, PHASES, phase, 0)
    for j in range(BITS):
        row_copy(j).wait_send()

    part[...] = jnp.zeros_like(part)
    wanted = [(0, 0), (0, 1), (0, 2), (1, 1), (1, 2), (2, 2)]
    for n, (i, j) in enumerate(wanted):
        for k in range(DIMS):
            part[pl.ds(n * DIMS + k, 1), :] = jnp.sum(
                q_v[i, k] * x_v[j + 1, k], axis=0, keepdims=True
            )
    for k in range(DIMS):
        part[pl.ds(6 * DIMS + k, 1), :] = jnp.sum(
            x_v[3, k] * w_v[2, k], axis=0, keepdims=True
        )
    sums = jnp.sum(part[...], axis=1, keepdims=True)
    eye = lax.broadcasted_iota(jnp.int32, part.shape, 0) == lax.broadcasted_iota(
        jnp.int32, part.shape, 1
    )
    row1[...] = jnp.sum(jnp.where(eye, sums, 0.0), axis=0, keepdims=True)

    def spread(count, source, target, send_sem, recv_sem, device):
        for o in range(1, count):
            pltpu.make_async_remote_copy(
                src_ref=source,
                dst_ref=target.at[count - 1 - o],
                send_sem=send_sem.at[o - 1],
                recv_sem=recv_sem.at[count - 1 - o],
                device_id=device(o),
            ).start()
        total = source[...]
        for e in range(count - 1):
            arrived = pltpu.make_async_remote_copy(
                src_ref=source,
                dst_ref=target.at[e],
                send_sem=send_sem.at[e],
                recv_sem=recv_sem.at[e],
                device_id=device(e + 1),
            )
            arrived.wait_recv()
            total = total + target[e]
        for e in range(count - 1):
            pltpu.make_async_remote_copy(
                src_ref=source,
                dst_ref=target.at[e],
                send_sem=send_sem.at[e],
                recv_sem=recv_sem.at[e],
                device_id=device(e + 1),
            ).wait_send()
        return total

    row2[...] = spread(N_SUB, row1, got1, a1_send, a1_recv, sub_dev)
    total = spread(
        N_DOM, row2, got2, a2_send, a2_recv, lambda o: {"dom": lax.rem(a + o, N_DOM)}
    )

    wide = jnp.broadcast_to(total, (8, TILE))
    values = [wide] + [pltpu.roll(wide, TILE - DIMS * n, 1) for n in range(1, 7)]
    gram = {}
    for (i, j), value in zip(wanted, values):
        gram[i, j] = gram[j, i] = value
    curve = {}
    for j in range(2):
        for i in range(3):
            curve[i, j] = curve[j, i] = gram[i, j + 1] + SHIFT * gram[i, j]
    curve[2, 2] = values[6]

    def form(table, vector):
        out = None
        for i in range(len(vector)):
            for j in range(i, len(vector)):
                term = vector[i] * vector[j] * table[i, j]
                term = term if i == j else 2.0 * term
                out = term if out is None else out + term
        return out

    one = jnp.ones((8, TILE), F32)
    rho = [one]
    along = [one]
    current = gram[0, 0]
    solved = [None] * 3
    for it in range(3):
        step = current / form(curve, along)
        for i, value in enumerate(along):
            moved_by = step * value
            solved[i] = moved_by if solved[i] is None else solved[i] + moved_by
        if it < 2:
            fresh = []
            for i in range(len(along) + 1):
                value = rho[i] if i < len(rho) else None
                if i < len(along):
                    value = value - step * (SHIFT * along[i])
                if i > 0:
                    less = step * along[i - 1]
                    value = -less if value is None else value - less
                fresh.append(value)
            rho = fresh
            following = form(gram, rho)
            ratio = following / current
            along = [
                value + ratio * along[i] if i < len(along) else value
                for i, value in enumerate(rho)
            ]
            current = following
    for k in range(DIMS):
        faired = x_v[0, k]
        left = q_v[0, k]
        for j in range(3):
            scale = solved[j][0:1, k : k + 1]
            faired = faired + scale * x_v[j + 1, k]
            left = left - scale * w_v[j, k]
        sol_o[k] = faired
        res_o[k] = left


def on_device(
    positions,
    mass,
    local_tiles,
    local_rows,
    local_cols,
    live_tiles,
    dom_tiles,
    dom_cols,
    dom_slots,
    dom_rows,
    sub_tiles,
    sub_cols,
    sub_slots,
    sub_rows,
    precond,
):
    vector = jax.ShapeDtypeStruct((DIMS, NB, TILE), F32)
    dma = pltpu.SemaphoreType.DMA
    solved, left = pl.pallas_call(
        kernel,
        out_shape=(vector, vector),
        in_specs=[pl.BlockSpec(memory_space=pl.ANY)] * 15,
        out_specs=(pl.BlockSpec(memory_space=pltpu.VMEM),) * 2,
        scratch_shapes=[
            pltpu.VMEM((PHASES, DIMS, NB, TILE), F32),
            pltpu.VMEM((PHASES, NB, 8, TILE), F32),
            pltpu.VMEM((3, DIMS, NB, TILE), F32),
            pltpu.VMEM((3, DIMS, NB, TILE), F32),
            pltpu.VMEM((NB, TILE), F32),
            pltpu.VMEM((2 * PAIRS, TILE, TILE), F32),
            pltpu.VMEM((PAIRS, 2 * TILE, 2 * TILE), BF16),
            pltpu.VMEM((ROWS_X * 8, TILE), F32),
            pltpu.VMEM((PAIRS * 16, TILE), F32),
            pltpu.VMEM((DIMS, NB, TILE), F32),
            pltpu.VMEM((PHASES, BITS, DIMS, NB, TILE), F32),
            pltpu.VMEM((PHASES, N_SUB - 1, DIMS, SS, TILE), F32),
            pltpu.VMEM((PHASES, N_SUB - 1, DIMS, SS, TILE), F32),
            pltpu.VMEM((NB, LT), BF16),
            pltpu.VMEM((NB, IFS), BF16),
            pltpu.VMEM((NB, IFD), BF16),
            pltpu.VMEM((1, LT), jnp.int32),
            pltpu.VMEM((1, IFS), jnp.int32),
            pltpu.VMEM((1, IFD), jnp.int32),
            pltpu.VMEM((4, TILE), jnp.int32),
            pltpu.VMEM((BITS, 4, TILE), jnp.int32),
            pltpu.VMEM((24, TILE), F32),
            pltpu.VMEM((1, TILE), F32),
            pltpu.VMEM((N_SUB - 1, 1, TILE), F32),
            pltpu.VMEM((1, TILE), F32),
            pltpu.VMEM((N_DOM - 1, 1, TILE), F32),
            pltpu.SMEM((LT,), jnp.int32),
            pltpu.SMEM((1,), jnp.int32),
            pltpu.SMEM((IFS,), jnp.int32),
            pltpu.SMEM((N_SUB * SS,), jnp.int32),
            pltpu.SMEM((IFD,), jnp.int32),
            pltpu.SMEM((BITS, 4, TILE), jnp.int32),
            pltpu.SMEM((2 * PAIR_P,), jnp.int32),
            dma((11,)),
            dma((2 * PAIRS // GROUP,)),
            dma((BITS,)),
            dma((BITS,)),
            dma,
            dma((PHASES, BITS)),
            dma((PHASES, BITS)),
            dma((PHASES, N_SUB - 1)),
            dma((PHASES, N_SUB - 1)),
            dma((N_SUB - 1,)),
            dma((N_SUB - 1,)),
            dma((N_DOM - 1,)),
            dma((N_DOM - 1,)),
        ],
        compiler_params=pltpu.CompilerParams(
            collective_id=0, has_side_effects=True, vmem_limit_bytes=56 * 1024 * 1024
        ),
    )(
        positions.reshape(DIMS, NB, TILE),
        mass.reshape(NB, TILE),
        local_tiles,
        local_rows,
        local_cols.reshape(1, LT),
        live_tiles,
        dom_tiles,
        dom_cols.reshape(1, IFD),
        dom_slots,
        dom_rows.reshape(4, TILE),
        sub_tiles,
        sub_cols.reshape(1, IFS),
        sub_slots,
        sub_rows,
        precond,
    )
    return solved.reshape(DIMS, NB * TILE), left.reshape(DIMS, NB * TILE)


def solution(mesh):
    flat = P(("dom", "sub"))
    cube = P(("dom", "sub"), None, None)
    vector = P(None, ("dom", "sub"))
    return jax.shard_map(
        on_device,
        mesh=mesh,
        in_specs=(
            vector,
            flat,
            cube,
            flat,
            flat,
            flat,
            cube,
            flat,
            flat,
            flat,
            cube,
            flat,
            flat,
            flat,
            cube,
        ),
        out_specs=(vector, vector),
        check_vma=False,
    )
```

profile of v0, /device:TPU:1, one launch (start us, length us, event | category | flops | bytes accessed | tf_op | source)
XLA Modules:
  0.0 48.3 jit_solution(17941226341045423460)
XLA Ops:
  1.3 1.5 %copy.23 = f32[1,3,32,128]{3,2,1,0:T(8,128)} copy(f32[1,3,32,128]{3,1,2,0:T(4,128)} %bitcast.16) | data formatting | bytes 98304
  2.7 44.0 %shard_map.158 = (f32[3,32,128]{2,1,0:T(8,128)}, f32[3,32,128]{2,1,0:T(8,128)}) custom-call(f32[3,32,128]{2,1,0:T(8,128)} %bitcast.15, f32[32,128]{1,0:T(8,128)} %bitcast.19, f32[64,128,128]{2,1,0:T(8,128)} %lt_h.1, s32[64]{0:T(128)} %lrow_h.1, s32[1,64]{1,0:T(1,128)} %bitcast.21, s32[1]{0:T(128)S(6)} %copy.24.live_h, f32[32,128,128]{2,1,0:T(8,128)} %dt_h.1, ...), custom_call_target="tpu_custom_call" | custom-call | tf_op jit(solution)/shard_map/pallas_call | solution.py:514
  46.8 1.5 %copy_bitcast_fusion = (f32[3,4096]{1,0:T(4,128)}, f32[3,4096]{1,0:T(4,128)}) fusion(f32[1,3,32,128]{3,2,1,0:T(8,128)} %bitcast.18, f32[1,3,32,128]{3,2,1,0:T(8,128)} %bitcast.17), kind=kLoop, calls=%fused_computation | loop fusion | bytes 196608 | tf_op jit(solution)/shard_map/reshape | solution.py:587
where the time goes:
time: 48.7 us; the launch traced here: 48.3 us
  Pallas kernels  44 us (90%)
  local copies, waits for them, and re-layouts  3.01 us (6%)
  between operations  1.28 us (3%)
    pallas_call x1, Pallas kernels, on_device(): pl.pallas_call(kernel, out_shape=(vector, vector), in_specs=[pl.BlockSpec...  44 us
    reshape x1, local copies, waits for them, and re-layouts, on_device(): return (solved.reshape(DIMS, NB * TILE), left.reshape(DIMS, NB * TILE))  1.54 us
    unnamed x1, local copies, waits for them, and re-layouts  1.46 us

commit v1 on v0

--- a/solution.py
+++ b/solution.py
@@ -54,6 +54,7 @@
     pt_h,
     sol_o,
     res_o,
+    pos_v,
     x_v,
     x3,
     q_v,
@@ -77,9 +78,7 @@
     drow_r,
     part,
     row1,
-    got1,
-    row2,
-    got2,
+    rows,
     lrow_m,
     live_m,
     sslot_m,
@@ -98,8 +97,6 @@
     ss_recv,
     a1_send,
     a1_recv,
-    a2_send,
-    a2_recv,
 ):
     a = lax.axis_index("dom")
     b = lax.axis_index("sub")
@@ -110,8 +107,14 @@
     def sub_dev(o):
         return {"sub": lax.rem(b + o, N_SUB)}
 
+    barrier = pltpu.get_barrier_semaphore()
+    for j in range(BITS):
+        pl.semaphore_signal(barrier, inc=1, device_id=dom_dev(j))
+    for o in range(1, N_SUB):
+        pl.semaphore_signal(barrier, inc=1, device_id=sub_dev(o))
+
     small = [
-        (pos_h, x_v.at[0]),
+        (pos_h, pos_v),
         (drow_h, drow_v),
         (mass_h, mass_v),
         (lrow_h, lrow_m),
@@ -141,13 +144,6 @@
     for copy in loads:
         copy.start()
 
-    barrier = pltpu.get_barrier_semaphore()
-    for j in range(BITS):
-        pl.semaphore_signal(barrier, inc=1, device_id=dom_dev(j))
-    for o in range(1, N_SUB):
-        pl.semaphore_signal(barrier, inc=1, device_id=sub_dev(o))
-    pl.semaphore_wait(barrier, BITS + N_SUB - 1)
-
     def dom_copy(p, j):
         return pltpu.make_async_remote_copy(
             src_ref=x_v.at[p],
@@ -196,8 +192,6 @@
                     pack[p, i, k, pl.ds(s, 1), :] = rows[k : k + 1]
             return carry
 
-        for k in range(DIMS):
-            x3[p, :, k, :] = x_v[p, k]
         lax.fori_loop(0, N_SUB - 1, gather, 0)
         for o in range(1, N_SUB):
             sub_copy(p, o).start()
@@ -216,7 +210,11 @@
             axis=0,
         ).astype(BF16)
         out = jnp.dot(
-            jnp.concatenate([left, left], axis=1), tb[pair], preferred_element_type=F32
+            jnp.concatenate([left, left], axis=1),
+            jnp.concatenate(
+                [tb[pair, 0, 0 : 2 * TILE, :], tb[pair, 1, 0 : 2 * TILE, :]], axis=1
+            ),
+            preferred_element_type=F32,
         )
         prod[pl.ds(pl.multiple_of(slot * 16, 16), 8), :] = out[0:8, 0:TILE]
         prod[pl.ds(pl.multiple_of(slot * 16 + 8, 8), 8), :] = out[8:16, TILE : 2 * TILE]
@@ -227,7 +225,7 @@
             multiply(pair, idx[2 * pair], idx[2 * pair + 1], pair)
             return carry
 
-        lax.fori_loop(0, count, body, 0, unroll=8)
+        lax.fori_loop(0, count, body, 0, unroll=True)
 
     def taken(first, count, k):
         return (
@@ -257,12 +255,16 @@
         return sums
 
     small[0].wait()
-    small[1].wait()
+    for c in range(NB):
+        x3[0, c, 0:DIMS, :] = pos_v[:, c * TILE : (c + 1) * TILE]
+    for k in range(DIMS):
+        x_v[0, k] = x3[0, :, k, :]
+    for copy in small[1:]:
+        copy.wait()
+    pl.semaphore_wait(barrier, BITS + N_SUB - 1)
+    send(0)
     for j in range(BITS):
         row_copy(j).start()
-    for copy in small[2:]:
-        copy.wait()
-    send(0)
 
     block_ids = lax.broadcasted_iota(jnp.int32, (NB, LT), 0)
     tile_ids = lax.broadcasted_iota(jnp.int32, (NB, LT), 1)
@@ -294,19 +296,20 @@
             tile = land[2 * i + half]
             high = tile.astype(BF16)
             low = (tile - high.astype(F32)).astype(BF16)
-            tb[i, 0:TILE, half * TILE : (half + 1) * TILE] = high
-            tb[i, TILE : 2 * TILE, half * TILE : (half + 1) * TILE] = low
+            tb[i, half, 0:TILE, :] = high
+            tb[i, half, TILE : 2 * TILE, :] = low
         return carry
 
-    for n, copy in enumerate(loads):
-        copy.wait()
-        lax.fori_loop(n * GROUP // 2, (n + 1) * GROUP // 2, convert, 0)
-
-    for j in range(BITS):
-        row_copy(j).wait_recv()
-    moved = pltpu.make_async_copy(drow_r, drow_m, ix_loc)
-    moved.start()
-    moved.wait()
+    def arrive(n, carry):
+        pltpu.make_async_copy(
+            lt_h.at[pl.ds(0, GROUP)],
+            land.at[pl.ds(n * GROUP, GROUP)],
+            tile_sem.at[n],
+        ).wait()
+        lax.fori_loop(0, GROUP // 2, lambda i, c: convert(n * GROUP // 2 + i, c), 0, unroll=4)
+        return carry
+
+    lax.fori_loop(0, 2 * PAIRS // GROUP, arrive, 0)
 
     def put_dom(t, carry):
         slot = dslot_m[t]
@@ -321,7 +324,8 @@
         idx[2 * PAIR_D + t] = BASE_D + bit * NB + block
         return carry
 
-    lax.fori_loop(0, IFD, put_dom, 0, unroll=8)
+    part[...] = jnp.zeros_like(part)
+    wanted = [(0, 0), (0, 1), (0, 2), (1, 1), (1, 2), (2, 2)]
 
     def phase(p, carry):
         @pl.when(p > 0)
@@ -330,6 +334,15 @@
 
         split(0, NB, [x_v[p, k] for k in range(DIMS)])
         run(PAIR_L, LT // 2)
+
+        @pl.when(p == PHASES - 1)
+        def _():
+            for n, (i, j) in enumerate(wanted):
+                for k in range(DIMS):
+                    part[pl.ds(n * DIMS + k, 1), :] = jnp.sum(
+                        q_v[i, k] * x_v[j + 1, k], axis=0, keepdims=True
+                    )
+
         for e in range(N_SUB - 1):
             sub_arrival(p, e).wait_recv()
             split(BASE_S + e * SS, SS, [got_s[p, e, k] for k in range(DIMS)])
@@ -338,6 +351,15 @@
         middle = combine(sel_s, PAIR_S, IFS)
         for k in range(DIMS):
             acc[k] = mass_v[...] * x_v[p, k] + (inner[k] + middle[k])
+        @pl.when(p == 0)
+        def _():
+            for j in range(BITS):
+                row_copy(j).wait_recv()
+            moved = pltpu.make_async_copy(drow_r, drow_m, ix_loc)
+            moved.start()
+            moved.wait()
+            lax.fori_loop(0, IFD, put_dom, 0, unroll=8)
+
         for j in range(BITS):
             dom_copy(p, j).wait_recv()
             split(BASE_D + j * NB, NB, [got_d[p, j, k] for k in range(DIMS)])
@@ -367,27 +389,15 @@
                 multiply(PAIR_P + i, 2 * i, 2 * i + 1, PAIR_P + i)
                 return carry
 
-            lax.fori_loop(0, NB // 2, body, 0, unroll=8)
+            lax.fori_loop(0, NB // 2, body, 0, unroll=True)
             for k in range(DIMS):
-                x_v[p + 1, k] = taken(PAIR_P, NB, k)
-
-        for j in range(BITS):
-            dom_copy(p, j).wait_send()
-        for o in range(1, N_SUB):
-            sub_copy(p, o).wait_send()
+                value = taken(PAIR_P, NB, k)
+                x_v[p + 1, k] = value
+                x3[p + 1, :, k, :] = value
+
         return carry
 
     lax.fori_loop(0, PHASES, phase, 0)
-    for j in range(BITS):
-        row_copy(j).wait_send()
-
-    part[...] = jnp.zeros_like(part)
-    wanted = [(0, 0), (0, 1), (0, 2), (1, 1), (1, 2), (2, 2)]
-    for n, (i, j) in enumerate(wanted):
-        for k in range(DIMS):
-            part[pl.ds(n * DIMS + k, 1), :] = jnp.sum(
-                q_v[i, k] * x_v[j + 1, k], axis=0, keepdims=True
-            )
     for k in range(DIMS):
         part[pl.ds(6 * DIMS + k, 1), :] = jnp.sum(
             x_v[3, k] * w_v[2, k], axis=0, keepdims=True
@@ -396,42 +406,35 @@
     eye = lax.broadcasted_iota(jnp.int32, part.shape, 0) == lax.broadcasted_iota(
         jnp.int32, part.shape, 1
     )
+    me = a * N_SUB + b
     row1[...] = jnp.sum(jnp.where(eye, sums, 0.0), axis=0, keepdims=True)
 
-    def spread(count, source, target, send_sem, recv_sem, device):
-        for o in range(1, count):
-            pltpu.make_async_remote_copy(
-                src_ref=source,
-                dst_ref=target.at[count - 1 - o],
-                send_sem=send_sem.at[o - 1],
-                recv_sem=recv_sem.at[count - 1 - o],
-                device_id=device(o),
-            ).start()
-        total = source[...]
-        for e in range(count - 1):
-            arrived = pltpu.make_async_remote_copy(
-                src_ref=source,
-                dst_ref=target.at[e],
-                send_sem=send_sem.at[e],
-                recv_sem=recv_sem.at[e],
-                device_id=device(e + 1),
-            )
-            arrived.wait_recv()
-            total = total + target[e]
-        for e in range(count - 1):
-            pltpu.make_async_remote_copy(
-                src_ref=source,
-                dst_ref=target.at[e],
-                send_sem=send_sem.at[e],
-                recv_sem=recv_sem.at[e],
-                device_id=device(e + 1),
-            ).wait_send()
-        return total
-
-    row2[...] = spread(N_SUB, row1, got1, a1_send, a1_recv, sub_dev)
-    total = spread(
-        N_DOM, row2, got2, a2_send, a2_recv, lambda o: {"dom": lax.rem(a + o, N_DOM)}
+    def row_to(i):
+        other = lax.rem(me + 1 + i, N_DOM * N_SUB)
+        return pltpu.make_async_remote_copy(
+            src_ref=row1,
+            dst_ref=rows.at[pl.ds(me, 1)],
+            send_sem=a1_send,
+            recv_sem=a1_recv,
+            device_id={"dom": other // N_SUB, "sub": lax.rem(other, N_SUB)},
+        )
+
+    def scatter(i, carry):
+        row_to(i).start()
+        return carry
+
+    lax.fori_loop(0, N_DOM * N_SUB - 1, scatter, 0, unroll=8)
+    rows[pl.ds(me, 1), :] = row1[...]
+    everyone = rows.at[pl.ds(0, N_DOM * N_SUB - 1)]
+    both = pltpu.make_async_remote_copy(
+        src_ref=everyone,
+        dst_ref=everyone,
+        send_sem=a1_send,
+        recv_sem=a1_recv,
+        device_id=sub_dev(1),
     )
+    both.wait_recv()
+    total = jnp.sum(rows[...], axis=0, keepdims=True)
 
     wide = jnp.broadcast_to(total, (8, TILE))
     values = [wide] + [pltpu.roll(wide, TILE - DIMS * n, 1) for n in range(1, 7)]
@@ -491,6 +494,15 @@
         sol_o[k] = faired
         res_o[k] = left
 
+    both.wait_send()
+    for j in range(BITS):
+        row_copy(j).wait_send()
+    for p in range(PHASES):
+        for j in range(BITS):
+            dom_copy(p, j).wait_send()
+        for o in range(1, N_SUB):
+            sub_copy(p, o).wait_send()
+
 
 def on_device(
     positions,
@@ -517,13 +529,14 @@
         in_specs=[pl.BlockSpec(memory_space=pl.ANY)] * 15,
         out_specs=(pl.BlockSpec(memory_space=pltpu.VMEM),) * 2,
         scratch_shapes=[
+            pltpu.VMEM((DIMS, NB * TILE), F32),
             pltpu.VMEM((PHASES, DIMS, NB, TILE), F32),
             pltpu.VMEM((PHASES, NB, 8, TILE), F32),
             pltpu.VMEM((3, DIMS, NB, TILE), F32),
             pltpu.VMEM((3, DIMS, NB, TILE), F32),
             pltpu.VMEM((NB, TILE), F32),
             pltpu.VMEM((2 * PAIRS, TILE, TILE), F32),
-            pltpu.VMEM((PAIRS, 2 * TILE, 2 * TILE), BF16),
+            pltpu.VMEM((PAIRS, 2, 2 * TILE + 16, TILE), BF16),
             pltpu.VMEM((ROWS_X * 8, TILE), F32),
             pltpu.VMEM((PAIRS * 16, TILE), F32),
             pltpu.VMEM((DIMS, NB, TILE), F32),
@@ -540,9 +553,7 @@
             pltpu.VMEM((BITS, 4, TILE), jnp.int32),
             pltpu.VMEM((24, TILE), F32),
             pltpu.VMEM((1, TILE), F32),
-            pltpu.VMEM((N_SUB - 1, 1, TILE), F32),
-            pltpu.VMEM((1, TILE), F32),
-            pltpu.VMEM((N_DOM - 1, 1, TILE), F32),
+            pltpu.VMEM((N_DOM * N_SUB, TILE), F32),
             pltpu.SMEM((LT,), jnp.int32),
             pltpu.SMEM((1,), jnp.int32),
             pltpu.SMEM((IFS,), jnp.int32),
@@ -559,16 +570,14 @@
             dma((PHASES, BITS)),
             dma((PHASES, N_SUB - 1)),
             dma((PHASES, N_SUB - 1)),
-            dma((N_SUB - 1,)),
-            dma((N_SUB - 1,)),
-            dma((N_DOM - 1,)),
-            dma((N_DOM - 1,)),
+            dma,
+            dma,
         ],
         compiler_params=pltpu.CompilerParams(
             collective_id=0, has_side_effects=True, vmem_limit_bytes=56 * 1024 * 1024
         ),
     )(
-        positions.reshape(DIMS, NB, TILE),
+        positions,
         mass.reshape(NB, TILE),
         local_tiles,
         local_rows,

time: 48.7 us -> 44.5 us (0.914)
  Pallas kernels: 44 us -> 41.5 us
  local copies, waits for them, and re-layouts: 3.01 us -> 1.54 us
    pallas_call x1, Pallas kernels: 44 us -> 41.5 us  [on_device(): pl.pallas_call(kernel, out_shape=(vector, vector), in_specs=[pl.BlockSpec...]
    unnamed x1 -> x0, local copies, waits for them, and re-layouts: 1.46 us -> none
where the time goes in v1:
time: 44.5 us; the launch traced here: 44.4 us
  Pallas kernels  41.5 us (93%)
  local copies, waits for them, and re-layouts  1.54 us (3%)
  between operations  1.29 us (3%)
    pallas_call x1, Pallas kernels, on_device(): pl.pallas_call(kernel, out_shape=(vector, vector), in_specs=[pl.BlockSpec...  41.5 us
    reshape x1, local copies, waits for them, and re-layouts, on_device(): return (solved.reshape(DIMS, NB * TILE), left.reshape(DIMS, NB * TILE))  1.54 us

profile of v1, /device:TPU:1, one launch (start us, length us, event | category | flops | bytes accessed | tf_op | source)
XLA Modules:
  0.0 44.4 jit_solution(5705846261486454812)
XLA Ops:
  1.3 41.5 %shard_map.158 = (f32[3,32,128]{2,1,0:T(8,128)}, f32[3,32,128]{2,1,0:T(8,128)}) custom-call(f32[3,4096]{1,0:T(4,128)} %pos_h.1, f32[32,128]{1,0:T(8,128)} %bitcast.13, f32[64,128,128]{2,1,0:T(8,128)} %lt_h.1, s32[64]{0:T(128)} %lrow_h.1, s32[1,64]{1,0:T(1,128)} %bitcast.15, s32[1]{0:T(128)S(6)} %copy.21.live_h, f32[32,128,128]{2,1,0:T(8,128)} %dt_h.1, ...), custom_call_target="tpu_custom_call" | custom-call | tf_op jit(solution)/shard_map/pallas_call | solution.py:526
  42.8 1.5 %copy_bitcast_fusion = (f32[3,4096]{1,0:T(4,128)}, f32[3,4096]{1,0:T(4,128)}) fusion(f32[1,3,32,128]{3,2,1,0:T(8,128)} %bitcast.12, f32[1,3,32,128]{3,2,1,0:T(8,128)} %bitcast.11), kind=kLoop, calls=%fused_computation | loop fusion | bytes 196608 | tf_op jit(solution)/shard_map/reshape | solution.py:596

commit v2 on v1

--- a/solution.py
+++ b/solution.py
@@ -27,6 +27,7 @@
 PAIR_P = PAIR_D + IFD // 2
 PAIRS = PAIR_P + NB // 2
 GROUP = 16
+EARLY = LT // GROUP
 
 BASE_D = NB
 BASE_S = NB + BITS * NB
@@ -86,6 +87,7 @@
     dslot_m,
     drow_m,
     idx,
+    spot,
     in_sem,
     tile_sem,
     ix_send,
@@ -141,7 +143,7 @@
                     tile_sem.at[len(loads)],
                 )
             )
-    for copy in loads:
+    for copy in loads[:EARLY]:
         copy.start()
 
     def dom_copy(p, j):
@@ -181,7 +183,7 @@
         )
 
     def send(p):
-        for j in range(BITS):
+        for j in (1, 3, 0, 2):
             dom_copy(p, j).start()
 
         def gather(i, carry):
@@ -193,7 +195,7 @@
             return carry
 
         lax.fori_loop(0, N_SUB - 1, gather, 0)
-        for o in range(1, N_SUB):
+        for o in (4, 3, 5, 2, 6, 1, 7):
             sub_copy(p, o).start()
 
     xg3 = xg.reshape(ROWS_X, 8, TILE)
@@ -262,9 +264,11 @@
     for copy in small[1:]:
         copy.wait()
     pl.semaphore_wait(barrier, BITS + N_SUB - 1)
-    send(0)
     for j in range(BITS):
         row_copy(j).start()
+    send(0)
+    for copy in loads[EARLY:]:
+        copy.start()
 
     block_ids = lax.broadcasted_iota(jnp.int32, (NB, LT), 0)
     tile_ids = lax.broadcasted_iota(jnp.int32, (NB, LT), 1)
@@ -291,27 +295,28 @@
     lax.fori_loop(0, LT, put_local, 0, unroll=8)
     lax.fori_loop(0, IFS, put_sub, 0, unroll=8)
 
-    def convert(i, carry):
+    def convert(i):
         for half in range(2):
             tile = land[2 * i + half]
             high = tile.astype(BF16)
             low = (tile - high.astype(F32)).astype(BF16)
             tb[i, half, 0:TILE, :] = high
             tb[i, half, TILE : 2 * TILE, :] = low
-        return carry
-
-    def arrive(n, carry):
-        pltpu.make_async_copy(
-            lt_h.at[pl.ds(0, GROUP)],
-            land.at[pl.ds(n * GROUP, GROUP)],
-            tile_sem.at[n],
-        ).wait()
-        lax.fori_loop(0, GROUP // 2, lambda i, c: convert(n * GROUP // 2 + i, c), 0, unroll=4)
-        return carry
-
-    lax.fori_loop(0, 2 * PAIRS // GROUP, arrive, 0)
-
-    def put_dom(t, carry):
+
+    def arrive(first, count):
+        def body(n, carry):
+            pltpu.make_async_copy(
+                lt_h.at[pl.ds(0, GROUP)],
+                land.at[pl.ds(n * GROUP, GROUP)],
+                tile_sem.at[n],
+            ).wait()
+            for i in range(GROUP // 2):
+                convert(n * GROUP // 2 + i)
+            return carry
+
+        lax.fori_loop(first * 2 // GROUP, (first + count) * 2 // GROUP, body, 0)
+
+    def put_place(t, carry):
         slot = dslot_m[t]
         other = jnp.bitwise_xor(jnp.right_shift(slot, 5), a)
         bit = (
@@ -320,69 +325,68 @@
             + (other >= 8).astype(jnp.int32)
         )
         place = a * SD + jnp.bitwise_and(slot, SD - 1)
-        block = drow_m[bit, jnp.right_shift(place, 7), jnp.bitwise_and(place, TILE - 1)]
+        spot[0, t] = bit
+        spot[1, t] = jnp.right_shift(place, 7)
+        spot[2, t] = jnp.bitwise_and(place, TILE - 1)
+        return carry
+
+    lax.fori_loop(0, IFD, put_place, 0, unroll=8)
+
+    def put_dom(t, carry):
+        bit = spot[0, t]
+        block = drow_m[bit, spot[1, t], spot[2, t]]
         idx[2 * PAIR_D + t] = BASE_D + bit * NB + block
         return carry
 
     part[...] = jnp.zeros_like(part)
     wanted = [(0, 0), (0, 1), (0, 2), (1, 1), (1, 2), (2, 2)]
 
-    def phase(p, carry):
-        @pl.when(p > 0)
-        def _():
+    moved = pltpu.make_async_copy(drow_r, drow_m, ix_loc)
+
+    def phase(p, first):
+        if first:
+            arrive(PAIR_L, LT // 2)
+        else:
             send(p)
-
         split(0, NB, [x_v[p, k] for k in range(DIMS)])
         run(PAIR_L, LT // 2)
-
-        @pl.when(p == PHASES - 1)
-        def _():
-            for n, (i, j) in enumerate(wanted):
-                for k in range(DIMS):
-                    part[pl.ds(n * DIMS + k, 1), :] = jnp.sum(
-                        q_v[i, k] * x_v[j + 1, k], axis=0, keepdims=True
-                    )
-
-        for e in range(N_SUB - 1):
+        if first:
+            for j in range(BITS):
+                row_copy(j).wait_recv()
+            moved.start()
+            arrive(PAIR_S, IFS // 2)
+        else:
+
+            @pl.when(p == PHASES - 1)
+            def _():
+                for n, (i, j) in enumerate(wanted):
+                    for k in range(DIMS):
+                        part[pl.ds(n * DIMS + k, 1), :] = jnp.sum(
+                            q_v[i, k] * x_v[j + 1, k], axis=0, keepdims=True
+                        )
+
+        for o in (7, 1, 2, 6, 3, 5, 4):
+            e = N_SUB - 1 - o
             sub_arrival(p, e).wait_recv()
             split(BASE_S + e * SS, SS, [got_s[p, e, k] for k in range(DIMS)])
         run(PAIR_S, IFS // 2)
+        if first:
+            arrive(PAIR_D, IFD // 2)
+            arrive(PAIR_P, NB // 2)
         inner = combine(sel_l, PAIR_L, LT)
         middle = combine(sel_s, PAIR_S, IFS)
         for k in range(DIMS):
             acc[k] = mass_v[...] * x_v[p, k] + (inner[k] + middle[k])
-        @pl.when(p == 0)
-        def _():
-            for j in range(BITS):
-                row_copy(j).wait_recv()
-            moved = pltpu.make_async_copy(drow_r, drow_m, ix_loc)
-            moved.start()
+        if first:
             moved.wait()
-            lax.fori_loop(0, IFD, put_dom, 0, unroll=8)
-
-        for j in range(BITS):
+            lax.fori_loop(0, IFD, put_dom, 0, unroll=True)
+        for j in (0, 2, 1, 3):
             dom_copy(p, j).wait_recv()
             split(BASE_D + j * NB, NB, [got_d[p, j, k] for k in range(DIMS)])
         run(PAIR_D, IFD // 2)
         outer = combine(sel_d, PAIR_D, IFD)
 
-        @pl.when(p == 0)
-        def _():
-            for k in range(DIMS):
-                q_v[0, k] = mass_v[...] * x_v[0, k] - (acc[k] + outer[k])
-
-        @pl.when(p > 0)
-        def _():
-            for k in range(DIMS):
-                w_v[p - 1, k] = acc[k] + outer[k]
-
-        @pl.when(jnp.logical_and(p > 0, p < PHASES - 1))
-        def _():
-            for k in range(DIMS):
-                q_v[p, k] = w_v[p - 1, k] - SHIFT * q_v[p - 1, k]
-
-        @pl.when(p < PHASES - 1)
-        def _():
+        def smooth():
             split(0, NB, [q_v[p, k] for k in range(DIMS)])
 
             def body(i, carry):
@@ -395,9 +399,26 @@
                 x_v[p + 1, k] = value
                 x3[p + 1, :, k, :] = value
 
+        if first:
+            for k in range(DIMS):
+                q_v[0, k] = mass_v[...] * x_v[0, k] - (acc[k] + outer[k])
+            smooth()
+        else:
+            for k in range(DIMS):
+                w_v[p - 1, k] = acc[k] + outer[k]
+
+            @pl.when(p < PHASES - 1)
+            def _():
+                for k in range(DIMS):
+                    q_v[p, k] = w_v[p - 1, k] - SHIFT * q_v[p - 1, k]
+                smooth()
+
+    def later(p, carry):
+        phase(p, False)
         return carry
 
-    lax.fori_loop(0, PHASES, phase, 0)
+    phase(0, True)
+    lax.fori_loop(1, PHASES, later, 0)
     for k in range(DIMS):
         part[pl.ds(6 * DIMS + k, 1), :] = jnp.sum(
             x_v[3, k] * w_v[2, k], axis=0, keepdims=True
@@ -409,21 +430,21 @@
     me = a * N_SUB + b
     row1[...] = jnp.sum(jnp.where(eye, sums, 0.0), axis=0, keepdims=True)
 
-    def row_to(i):
-        other = lax.rem(me + 1 + i, N_DOM * N_SUB)
-        return pltpu.make_async_remote_copy(
+    def hops(m):
+        return sum((0, 1, 2, 1)[(m >> at) & 3] for at in (1, 3, 5))
+
+    for m in sorted(range(1, N_DOM * N_SUB), key=lambda m: -hops(m)):
+        other = jnp.bitwise_xor(me, m)
+        pltpu.make_async_remote_copy(
             src_ref=row1,
             dst_ref=rows.at[pl.ds(me, 1)],
             send_sem=a1_send,
             recv_sem=a1_recv,
-            device_id={"dom": other // N_SUB, "sub": lax.rem(other, N_SUB)},
-        )
-
-    def scatter(i, carry):
-        row_to(i).start()
-        return carry
-
-    lax.fori_loop(0, N_DOM * N_SUB - 1, scatter, 0, unroll=8)
+            device_id={
+                "dom": jnp.right_shift(other, 3),
+                "sub": jnp.bitwise_and(other, N_SUB - 1),
+            },
+        ).start()
     rows[pl.ds(me, 1), :] = row1[...]
     everyone = rows.at[pl.ds(0, N_DOM * N_SUB - 1)]
     both = pltpu.make_async_remote_copy(
@@ -561,6 +582,7 @@
             pltpu.SMEM((IFD,), jnp.int32),
             pltpu.SMEM((BITS, 4, TILE), jnp.int32),
             pltpu.SMEM((2 * PAIR_P,), jnp.int32),
+            pltpu.SMEM((3, IFD), jnp.int32),
             dma((11,)),
             dma((2 * PAIRS // GROUP,)),
             dma((BITS,)),

time: 44.5 us -> 41 us (0.921)
  Pallas kernels: 41.5 us -> 37.9 us
    pallas_call x1, Pallas kernels: 41.5 us -> 37.9 us  [on_device(): pl.pallas_call(kernel, out_shape=(vector, vector), in_specs=[pl.BlockSpec...]
where the time goes in v2:
time: 41 us; the launch traced here: 40.8 us
  Pallas kernels  37.9 us (92%)
  local copies, waits for them, and re-layouts  1.54 us (4%)
  between operations  1.29 us (3%)
    pallas_call x1, Pallas kernels, on_device(): pl.pallas_call(kernel, out_shape=(vector, vector), in_specs=[pl.BlockSpec...  37.9 us
    reshape x1, local copies, waits for them, and re-layouts, on_device(): return (solved.reshape(DIMS, NB * TILE), left.reshape(DIMS, NB * TILE))  1.54 us

profile of v2, /device:TPU:1, one launch (start us, length us, event | category | flops | bytes accessed | tf_op | source)
XLA Modules:
  0.0 40.8 jit_solution(10023720937759423307)
XLA Ops:
  1.3 37.9 %shard_map.158 = (f32[3,32,128]{2,1,0:T(8,128)}, f32[3,32,128]{2,1,0:T(8,128)}) custom-call(f32[3,4096]{1,0:T(4,128)} %pos_h.1, f32[32,128]{1,0:T(8,128)} %bitcast.13, f32[64,128,128]{2,1,0:T(8,128)} %lt_h.1, s32[64]{0:T(128)} %lrow_h.1, s32[1,64]{1,0:T(1,128)} %bitcast.15, s32[1]{0:T(128)S(6)} %copy.21.live_h, f32[32,128,128]{2,1,0:T(8,128)} %dt_h.1, ...), custom_call_target="tpu_custom_call" | custom-call | tf_op jit(solution)/shard_map/pallas_call | solution.py:547
  39.2 1.5 %copy_bitcast_fusion = (f32[3,4096]{1,0:T(4,128)}, f32[3,4096]{1,0:T(4,128)}) fusion(f32[1,3,32,128]{3,2,1,0:T(8,128)} %bitcast.12, f32[1,3,32,128]{3,2,1,0:T(8,128)} %bitcast.11), kind=kLoop, calls=%fused_computation | loop fusion | bytes 196608 | tf_op jit(solution)/shard_map/reshape | solution.py:618

commit v3 on v2

--- a/solution.py
+++ b/solution.py
@@ -70,15 +70,17 @@
     got_s,
     pack,
     sel_l,
-    sel_s,
-    sel_d,
+    sel_r,
+    held,
     lcol_v,
     scol_v,
     dcol_v,
     drow_v,
     drow_r,
     part,
-    row1,
+    bent,
+    last_v,
+    row,
     rows,
     lrow_m,
     live_m,
@@ -86,6 +88,8 @@
     srow_m,
     dslot_m,
     drow_m,
+    scol_m,
+    dcol_m,
     idx,
     spot,
     in_sem,
@@ -97,8 +101,8 @@
     sd_recv,
     ss_send,
     ss_recv,
-    a1_send,
-    a1_recv,
+    row_send,
+    row_recv,
 ):
     a = lax.axis_index("dom")
     b = lax.axis_index("sub")
@@ -110,8 +114,8 @@
         return {"sub": lax.rem(b + o, N_SUB)}
 
     barrier = pltpu.get_barrier_semaphore()
-    for j in range(BITS):
-        pl.semaphore_signal(barrier, inc=1, device_id=dom_dev(j))
+    for m in (1, 2, 3, 4, 8, 12):
+        pl.semaphore_signal(barrier, inc=1, device_id={"dom": jnp.bitwise_xor(a, m)})
     for o in range(1, N_SUB):
         pl.semaphore_signal(barrier, inc=1, device_id=sub_dev(o))
 
@@ -127,6 +131,8 @@
         (lcol_h, lcol_v),
         (scol_h, scol_v),
         (dcol_h, dcol_v),
+        (scol_h, scol_m),
+        (dcol_h, dcol_m),
     ]
     small = [
         pltpu.make_async_copy(src, dst, in_sem.at[i]) for i, (src, dst) in enumerate(small)
@@ -186,17 +192,19 @@
         for j in (1, 3, 0, 2):
             dom_copy(p, j).start()
 
-        def gather(i, carry):
+        if isinstance(p, int) and p == 0:
+            for copy in small[2:]:
+                copy.wait()
+        order = (4, 3, 5, 2, 6, 1, 7)
+        for n, o in enumerate(order):
             for s in range(SS):
-                block = srow_m[lax.rem(b + i + 1, N_SUB) * SS + s]
-                rows = x3[p, block]
+                block = srow_m[lax.rem(b + o, N_SUB) * SS + s]
+                values = x3[p, block]
                 for k in range(DIMS):
-                    pack[p, i, k, pl.ds(s, 1), :] = rows[k : k + 1]
-            return carry
-
-        lax.fori_loop(0, N_SUB - 1, gather, 0)
-        for o in (4, 3, 5, 2, 6, 1, 7):
-            sub_copy(p, o).start()
+                    pack[p, o - 1, k, pl.ds(s, 1), :] = values[k : k + 1]
+            if n:
+                sub_copy(p, order[n - 1]).start()
+        sub_copy(p, order[-1]).start()
 
     xg3 = xg.reshape(ROWS_X, 8, TILE)
 
@@ -235,7 +243,7 @@
             + prod[pl.ds(first * 16 + DIMS + k, count, stride=8), :]
         )
 
-    def combine(select, first, count):
+    def terms_of(first, count):
         terms = []
         for k in range(DIMS):
             value = taken(first, count, k)
@@ -243,9 +251,10 @@
             rest = value - high.astype(F32)
             middle = rest.astype(BF16)
             terms += [high, middle, (rest - middle.astype(F32)).astype(BF16)]
-        out = jnp.dot(
-            select[...], jnp.concatenate(terms, axis=1), preferred_element_type=F32
-        )
+        return jnp.concatenate(terms, axis=1)
+
+    def combine(select, terms):
+        out = jnp.dot(select[...], terms, preferred_element_type=F32)
         sums = []
         for k in range(DIMS):
             at = 3 * k * TILE
@@ -256,16 +265,15 @@
             )
         return sums
 
+    small[1].wait()
+    pl.semaphore_wait(barrier, 6 + N_SUB - 1)
+    for j in range(BITS):
+        row_copy(j).start()
     small[0].wait()
     for c in range(NB):
         x3[0, c, 0:DIMS, :] = pos_v[:, c * TILE : (c + 1) * TILE]
     for k in range(DIMS):
         x_v[0, k] = x3[0, :, k, :]
-    for copy in small[1:]:
-        copy.wait()
-    pl.semaphore_wait(barrier, BITS + N_SUB - 1)
-    for j in range(BITS):
-        row_copy(j).start()
     send(0)
     for copy in loads[EARLY:]:
         copy.start()
@@ -274,10 +282,10 @@
     tile_ids = lax.broadcasted_iota(jnp.int32, (NB, LT), 1)
     hit = jnp.logical_and(lcol_v[...] == block_ids, tile_ids < live_m[0])
     sel_l[...] = jnp.where(hit, 1.0, 0.0).astype(BF16)
-    sel_s[...] = jnp.where(
+    sel_r[:, 0:IFS] = jnp.where(
         scol_v[...] == lax.broadcasted_iota(jnp.int32, (NB, IFS), 0), 1.0, 0.0
     ).astype(BF16)
-    sel_d[...] = jnp.where(
+    sel_r[:, IFS : IFS + IFD] = jnp.where(
         dcol_v[...] == lax.broadcasted_iota(jnp.int32, (NB, IFD), 0), 1.0, 0.0
     ).astype(BF16)
     xg[...] = jnp.zeros_like(xg)
@@ -340,10 +348,68 @@
 
     part[...] = jnp.zeros_like(part)
     wanted = [(0, 0), (0, 1), (0, 2), (1, 1), (1, 2), (2, 2)]
-
     moved = pltpu.make_async_copy(drow_r, drow_m, ix_loc)
-
-    def phase(p, first):
+    me = a * N_SUB + b
+    count = N_DOM * N_SUB
+
+    def hops(m):
+        return sum((0, 1, 2, 1)[(m >> at) & 3] for at in (1, 3, 5))
+
+    def row_to(which, m):
+        other = jnp.bitwise_xor(me, m)
+        return pltpu.make_async_remote_copy(
+            src_ref=row.at[which],
+            dst_ref=rows.at[which, pl.ds(me, 1)],
+            send_sem=row_send.at[which],
+            recv_sem=row_recv.at[which],
+            device_id={
+                "dom": jnp.right_shift(other, 3),
+                "sub": jnp.bitwise_and(other, N_SUB - 1),
+            },
+        )
+
+    def row_all(which):
+        everyone = rows.at[which, pl.ds(0, count - 1)]
+        return pltpu.make_async_remote_copy(
+            src_ref=everyone,
+            dst_ref=everyone,
+            send_sem=row_send.at[which],
+            recv_sem=row_recv.at[which],
+            device_id=sub_dev(1),
+        )
+
+    def to_row(which, table):
+        sums = jnp.sum(table, axis=1, keepdims=True)
+        eye = lax.broadcasted_iota(jnp.int32, table.shape, 0) == lax.broadcasted_iota(
+            jnp.int32, table.shape, 1
+        )
+        value = jnp.sum(jnp.where(eye, sums, 0.0), axis=0, keepdims=True)
+        row[which] = value
+        rows[which, pl.ds(me, 1), :] = value
+
+    def early_rows():
+        for n, (i, j) in enumerate(wanted):
+            for k in range(DIMS):
+                part[pl.ds(n * DIMS + k, 1), :] = jnp.sum(
+                    q_v[i, k] * x_v[j + 1, k], axis=0, keepdims=True
+                )
+        to_row(0, part[...])
+
+        def body(i, carry):
+            row_to(0, i + 1).start()
+            return carry
+
+        lax.fori_loop(0, count - 1, body, 0, unroll=4)
+
+    def met(p, first, count, columns):
+        total = None
+        for t in range(count):
+            at = (2 * first + t) * 8
+            term = x3[p, columns[0, t]] * prod[at : at + 8, :]
+            total = term if total is None else total + term
+        return total
+
+    def phase(p, first, last):
         if first:
             arrive(PAIR_L, LT // 2)
         else:
@@ -355,16 +421,13 @@
                 row_copy(j).wait_recv()
             moved.start()
             arrive(PAIR_S, IFS // 2)
-        else:
-
-            @pl.when(p == PHASES - 1)
-            def _():
-                for n, (i, j) in enumerate(wanted):
-                    for k in range(DIMS):
-                        part[pl.ds(n * DIMS + k, 1), :] = jnp.sum(
-                            q_v[i, k] * x_v[j + 1, k], axis=0, keepdims=True
-                        )
-
+        inner = combine(sel_l, terms_of(PAIR_L, LT))
+        for k in range(DIMS):
+            acc[k] = mass_v[...] * x_v[p, k] + inner[k]
+        if last:
+            early_rows()
+            for k in range(DIMS):
+                x3[p, :, DIMS + k, :] = x_v[p, k]
         for o in (7, 1, 2, 6, 3, 5, 4):
             e = N_SUB - 1 - o
             sub_arrival(p, e).wait_recv()
@@ -373,10 +436,13 @@
         if first:
             arrive(PAIR_D, IFD // 2)
             arrive(PAIR_P, NB // 2)
-        inner = combine(sel_l, PAIR_L, LT)
-        middle = combine(sel_s, PAIR_S, IFS)
-        for k in range(DIMS):
-            acc[k] = mass_v[...] * x_v[p, k] + (inner[k] + middle[k])
+        held[...] = terms_of(PAIR_S, IFS)
+        if last:
+            bent[...] = met(p, PAIR_S, IFS, scol_m)
+            for k in range(DIMS):
+                bent[k : k + 1, :] += jnp.sum(
+                    acc[k] * x_v[p, k], axis=0, keepdims=True
+                )
         if first:
             moved.wait()
             lax.fori_loop(0, IFD, put_dom, 0, unroll=True)
@@ -384,81 +450,42 @@
             dom_copy(p, j).wait_recv()
             split(BASE_D + j * NB, NB, [got_d[p, j, k] for k in range(DIMS)])
         run(PAIR_D, IFD // 2)
-        outer = combine(sel_d, PAIR_D, IFD)
-
-        def smooth():
+        if last:
+            whole = bent[...] + met(p, PAIR_D, IFD, dcol_m)
+            to_row(1, whole[0:DIMS] + whole[DIMS : 2 * DIMS])
+            for m in sorted(range(1, count), key=lambda m: -hops(m)):
+                row_to(1, m).start()
+        outer = combine(
+            sel_r, jnp.concatenate([held[...], terms_of(PAIR_D, IFD)], axis=0)
+        )
+        for k in range(DIMS):
+            value = acc[k] + outer[k]
+            if first:
+                q_v[0, k] = mass_v[...] * x_v[0, k] - value
+            else:
+                w_v[p - 1, k] = value
+                if not last:
+                    q_v[p, k] = value - SHIFT * q_v[p - 1, k]
+        if not last:
             split(0, NB, [q_v[p, k] for k in range(DIMS)])
-
-            def body(i, carry):
+            for i in range(NB // 2):
                 multiply(PAIR_P + i, 2 * i, 2 * i + 1, PAIR_P + i)
-                return carry
-
-            lax.fori_loop(0, NB // 2, body, 0, unroll=True)
             for k in range(DIMS):
                 value = taken(PAIR_P, NB, k)
                 x_v[p + 1, k] = value
                 x3[p + 1, :, k, :] = value
 
-        if first:
-            for k in range(DIMS):
-                q_v[0, k] = mass_v[...] * x_v[0, k] - (acc[k] + outer[k])
-            smooth()
-        else:
-            for k in range(DIMS):
-                w_v[p - 1, k] = acc[k] + outer[k]
-
-            @pl.when(p < PHASES - 1)
-            def _():
-                for k in range(DIMS):
-                    q_v[p, k] = w_v[p - 1, k] - SHIFT * q_v[p - 1, k]
-                smooth()
-
     def later(p, carry):
-        phase(p, False)
+        phase(p, False, False)
         return carry
 
-    phase(0, True)
-    lax.fori_loop(1, PHASES, later, 0)
-    for k in range(DIMS):
-        part[pl.ds(6 * DIMS + k, 1), :] = jnp.sum(
-            x_v[3, k] * w_v[2, k], axis=0, keepdims=True
-        )
-    sums = jnp.sum(part[...], axis=1, keepdims=True)
-    eye = lax.broadcasted_iota(jnp.int32, part.shape, 0) == lax.broadcasted_iota(
-        jnp.int32, part.shape, 1
-    )
-    me = a * N_SUB + b
-    row1[...] = jnp.sum(jnp.where(eye, sums, 0.0), axis=0, keepdims=True)
-
-    def hops(m):
-        return sum((0, 1, 2, 1)[(m >> at) & 3] for at in (1, 3, 5))
-
-    for m in sorted(range(1, N_DOM * N_SUB), key=lambda m: -hops(m)):
-        other = jnp.bitwise_xor(me, m)
-        pltpu.make_async_remote_copy(
-            src_ref=row1,
-            dst_ref=rows.at[pl.ds(me, 1)],
-            send_sem=a1_send,
-            recv_sem=a1_recv,
-            device_id={
-                "dom": jnp.right_shift(other, 3),
-                "sub": jnp.bitwise_and(other, N_SUB - 1),
-            },
-        ).start()
-    rows[pl.ds(me, 1), :] = row1[...]
-    everyone = rows.at[pl.ds(0, N_DOM * N_SUB - 1)]
-    both = pltpu.make_async_remote_copy(
-        src_ref=everyone,
-        dst_ref=everyone,
-        send_sem=a1_send,
-        recv_sem=a1_recv,
-        device_id=sub_dev(1),
-    )
-    both.wait_recv()
-    total = jnp.sum(rows[...], axis=0, keepdims=True)
-
-    wide = jnp.broadcast_to(total, (8, TILE))
-    values = [wide] + [pltpu.roll(wide, TILE - DIMS * n, 1) for n in range(1, 7)]
+    phase(0, True, False)
+    lax.fori_loop(1, PHASES - 1, later, 0)
+    phase(PHASES - 1, False, True)
+
+    row_all(0).wait_recv()
+    wide = jnp.broadcast_to(jnp.sum(rows[0], axis=0, keepdims=True), (8, TILE))
+    values = [wide] + [pltpu.roll(wide, TILE - DIMS * n, 1) for n in range(1, 6)]
     gram = {}
     for (i, j), value in zip(wanted, values):
         gram[i, j] = gram[j, i] = value
@@ -466,56 +493,72 @@
     for j in range(2):
         for i in range(3):
             curve[i, j] = curve[j, i] = gram[i, j + 1] + SHIFT * gram[i, j]
-    curve[2, 2] = values[6]
 
     def form(table, vector):
         out = None
         for i in range(len(vector)):
             for j in range(i, len(vector)):
-                term = vector[i] * vector[j] * table[i, j]
-                term = term if i == j else 2.0 * term
-                out = term if out is None else out + term
+                if (i, j) in table:
+                    term = vector[i] * vector[j] * table[i, j]
+                    term = term if i == j else 2.0 * term
+                    out = term if out is None else out + term
         return out
 
     one = jnp.ones((8, TILE), F32)
     rho = [one]
     along = [one]
     current = gram[0, 0]
-    solved = [None] * 3
-    for it in range(3):
+    solved = []
+    for it in range(2):
         step = current / form(curve, along)
         for i, value in enumerate(along):
-            moved_by = step * value
-            solved[i] = moved_by if solved[i] is None else solved[i] + moved_by
-        if it < 2:
-            fresh = []
-            for i in range(len(along) + 1):
-                value = rho[i] if i < len(rho) else None
-                if i < len(along):
-                    value = value - step * (SHIFT * along[i])
-                if i > 0:
-                    less = step * along[i - 1]
-                    value = -less if value is None else value - less
-                fresh.append(value)
-            rho = fresh
-            following = form(gram, rho)
-            ratio = following / current
-            along = [
-                value + ratio * along[i] if i < len(along) else value
-                for i, value in enumerate(rho)
-            ]
-            current = following
+            if i < len(solved):
+                solved[i] = solved[i] + step * value
+            else:
+                solved.append(step * value)
+        fresh = []
+        for i in range(len(along) + 1):
+            value = rho[i] if i < len(rho) else None
+            if i < len(along):
+                value = value - step * (SHIFT * along[i])
+            if i > 0:
+                less = step * along[i - 1]
+                value = -less if value is None else value - less
+            fresh.append(value)
+        rho = fresh
+        following = form(gram, rho)
+        ratio = following / current
+        along = [
+            value + ratio * along[i] if i < len(along) else value
+            for i, value in enumerate(rho)
+        ]
+        current = following
+    known = form(curve, along)
+    square = along[2] * along[2]
     for k in range(DIMS):
-        faired = x_v[0, k]
-        left = q_v[0, k]
+        faired, left = x_v[0, k], q_v[0, k]
+        turn, lift = None, None
         for j in range(3):
-            scale = solved[j][0:1, k : k + 1]
-            faired = faired + scale * x_v[j + 1, k]
-            left = left - scale * w_v[j, k]
-        sol_o[k] = faired
-        res_o[k] = left
-
-    both.wait_send()
+            scale = along[j][0:1, k : k + 1]
+            turn = scale * x_v[j + 1, k] if j == 0 else turn + scale * x_v[j + 1, k]
+            lift = scale * w_v[j, k] if j == 0 else lift + scale * w_v[j, k]
+            if j < 2:
+                scale = solved[j][0:1, k : k + 1]
+                faired = faired + scale * x_v[j + 1, k]
+                left = left - scale * w_v[j, k]
+        last_v[0, k] = faired
+        last_v[1, k] = turn
+        last_v[2, k] = left
+        last_v[3, k] = lift
+    row_all(1).wait_recv()
+    step = current / (known + square * jnp.sum(rows[1], axis=0, keepdims=True))
+    for k in range(DIMS):
+        scale = step[0:1, k : k + 1]
+        sol_o[k] = last_v[0, k] + scale * last_v[1, k]
+        res_o[k] = last_v[2, k] - scale * last_v[3, k]
+
+    for which in range(2):
+        row_all(which).wait_send()
     for j in range(BITS):
         row_copy(j).wait_send()
     for p in range(PHASES):
@@ -546,7 +589,7 @@
     dma = pltpu.SemaphoreType.DMA
     solved, left = pl.pallas_call(
         kernel,
-        out_shape=(vector, vector),
+        out_shape=(pltpu.VMEM((DIMS, NB, TILE), F32),) * 2,
         in_specs=[pl.BlockSpec(memory_space=pl.ANY)] * 15,
         out_specs=(pl.BlockSpec(memory_space=pltpu.VMEM),) * 2,
         scratch_shapes=[
@@ -565,25 +608,29 @@
             pltpu.VMEM((PHASES, N_SUB - 1, DIMS, SS, TILE), F32),
             pltpu.VMEM((PHASES, N_SUB - 1, DIMS, SS, TILE), F32),
             pltpu.VMEM((NB, LT), BF16),
-            pltpu.VMEM((NB, IFS), BF16),
-            pltpu.VMEM((NB, IFD), BF16),
+            pltpu.VMEM((NB, IFS + IFD), BF16),
+            pltpu.VMEM((IFS, 9 * TILE), BF16),
             pltpu.VMEM((1, LT), jnp.int32),
             pltpu.VMEM((1, IFS), jnp.int32),
             pltpu.VMEM((1, IFD), jnp.int32),
             pltpu.VMEM((4, TILE), jnp.int32),
             pltpu.VMEM((BITS, 4, TILE), jnp.int32),
             pltpu.VMEM((24, TILE), F32),
-            pltpu.VMEM((1, TILE), F32),
-            pltpu.VMEM((N_DOM * N_SUB, TILE), F32),
+            pltpu.VMEM((8, TILE), F32),
+            pltpu.VMEM((4, DIMS, NB, TILE), F32),
+            pltpu.VMEM((2, 1, TILE), F32),
+            pltpu.VMEM((2, N_DOM * N_SUB, TILE), F32),
             pltpu.SMEM((LT,), jnp.int32),
             pltpu.SMEM((1,), jnp.int32),
             pltpu.SMEM((IFS,), jnp.int32),
             pltpu.SMEM((N_SUB * SS,), jnp.int32),
             pltpu.SMEM((IFD,), jnp.int32),
             pltpu.SMEM((BITS, 4, TILE), jnp.int32),
+            pltpu.SMEM((1, IFS), jnp.int32),
+            pltpu.SMEM((1, IFD), jnp.int32),
             pltpu.SMEM((2 * PAIR_P,), jnp.int32),
             pltpu.SMEM((3, IFD), jnp.int32),
-            dma((11,)),
+            dma((13,)),
             dma((2 * PAIRS // GROUP,)),
             dma((BITS,)),
             dma((BITS,)),
@@ -592,8 +639,8 @@
             dma((PHASES, BITS)),
             dma((PHASES, N_SUB - 1)),
             dma((PHASES, N_SUB - 1)),
-            dma,
-            dma,
+            dma((2,)),
+            dma((2,)),
         ],
         compiler_params=pltpu.CompilerParams(
             collective_id=0, has_side_effects=True, vmem_limit_bytes=56 * 1024 * 1024

time: 41 us -> 38.8 us (0.946)
  Pallas kernels: 37.9 us -> 36.6 us
  local copies, waits for them, and re-layouts: 1.54 us -> 0.72 us
    pallas_call x1, Pallas kernels: 37.9 us -> 36.6 us  [on_device(): pl.pallas_call(kernel, out_shape=(pltpu.VMEM((DIMS, NB, TILE), F32),) * 2...]
    reshape x1, local copies, waits for them, and re-layouts: 1.54 us -> 0.72 us  [on_device(): return (solved.reshape(DIMS, NB * TILE), left.reshape(DIMS, NB * TILE))]
where the time goes in v3:
time: 38.8 us; the launch traced here: 38.7 us
  Pallas kernels  36.6 us (94%)
  between operations  1.29 us (3%)
  local copies, waits for them, and re-layouts  0.72 us (2%)
    pallas_call x1, Pallas kernels, on_device(): pl.pallas_call(kernel, out_shape=(pltpu.VMEM((DIMS, NB, TILE), F32),) * 2...  36.6 us

profile of v3, /device:TPU:1, one launch (start us, length us, event | category | flops | bytes accessed | tf_op | source)
XLA Modules:
  0.0 38.7 jit_solution(5458714454157439350)
XLA Ops:
  1.3 36.6 %shard_map.158 = (f32[3,32,128]{2,1,0:T(8,128)S(1)}, f32[3,32,128]{2,1,0:T(8,128)S(1)}) custom-call(f32[3,4096]{1,0:T(4,128)} %pos_h.1, f32[32,128]{1,0:T(8,128)} %bitcast.13, f32[64,128,128]{2,1,0:T(8,128)} %lt_h.1, s32[64]{0:T(128)} %lrow_h.1, s32[1,64]{1,0:T(1,128)} %bitcast.15, s32[1]{0:T(128)S(6)} %copy.21.live_h, f32[32,128,128]{2,1,0:T(8,128)} %dt_h.1, ...), custom_call_target="tpu_custom_call" | custom-call | tf_op jit(solution)/shard_map/pallas_call | solution.py:590
  37.9 0.7 %copy_bitcast_fusion = (f32[3,4096]{1,0:T(4,128)}, f32[3,4096]{1,0:T(4,128)}) fusion(f32[1,3,32,128]{3,2,1,0:T(8,128)S(1)} %bitcast.12, f32[1,3,32,128]{3,2,1,0:T(8,128)S(1)} %bitcast.11), kind=kLoop, calls=%fused_computation | loop fusion | bytes 196608 | tf_op jit(solution)/shard_map/reshape | solution.py:665

commit v4 on v3

--- a/solution.py
+++ b/solution.py
@@ -28,6 +28,10 @@
 PAIRS = PAIR_P + NB // 2
 GROUP = 16
 EARLY = LT // GROUP
+
+FAR = (4, 5, 6, 7)
+NEAR = (2, 3, 1)
+NEAR_TILES = IFS - len(FAR) * SS
 
 BASE_D = NB
 BASE_S = NB + BITS * NB
@@ -75,6 +79,8 @@
     lcol_v,
     scol_v,
     dcol_v,
+    sslot_v,
+    tab_v,
     drow_v,
     drow_r,
     part,
@@ -84,12 +90,11 @@
     rows,
     lrow_m,
     live_m,
-    sslot_m,
     srow_m,
     dslot_m,
     drow_m,
-    scol_m,
     dcol_m,
+    tab_m,
     idx,
     spot,
     in_sem,
@@ -97,6 +102,7 @@
     ix_send,
     ix_recv,
     ix_loc,
+    tab_sem,
     sd_send,
     sd_recv,
     ss_send,
@@ -110,14 +116,8 @@
     def dom_dev(j):
         return {"dom": jnp.bitwise_xor(a, 1 << j)}
 
-    def sub_dev(o):
-        return {"sub": lax.rem(b + o, N_SUB)}
-
-    barrier = pltpu.get_barrier_semaphore()
-    for m in (1, 2, 3, 4, 8, 12):
-        pl.semaphore_signal(barrier, inc=1, device_id={"dom": jnp.bitwise_xor(a, m)})
-    for o in range(1, N_SUB):
-        pl.semaphore_signal(barrier, inc=1, device_id=sub_dev(o))
+    def sub_dev(m):
+        return {"sub": jnp.bitwise_xor(b, m)}
 
     small = [
         (pos_h, pos_v),
@@ -125,13 +125,12 @@
         (mass_h, mass_v),
         (lrow_h, lrow_m),
         (live_h, live_m),
-        (sslot_h, sslot_m),
+        (sslot_h, sslot_v),
         (srow_h, srow_m),
         (dslot_h, dslot_m),
         (lcol_h, lcol_v),
         (scol_h, scol_v),
         (dcol_h, dcol_v),
-        (scol_h, scol_m),
         (dcol_h, dcol_m),
     ]
     small = [
@@ -149,6 +148,12 @@
                     tile_sem.at[len(loads)],
                 )
             )
+    barrier = pltpu.get_barrier_semaphore()
+    for m in (1, 2, 3, 4, 8, 12):
+        pl.semaphore_signal(barrier, inc=1, device_id={"dom": jnp.bitwise_xor(a, m)})
+    for o in range(1, N_SUB):
+        pl.semaphore_signal(barrier, inc=1, device_id=sub_dev(o))
+
     for copy in loads[:EARLY]:
         copy.start()
 
@@ -161,22 +166,13 @@
             device_id=dom_dev(j),
         )
 
-    def sub_copy(p, o):
+    def sub_copy(p, m):
         return pltpu.make_async_remote_copy(
-            src_ref=pack.at[p, o - 1],
-            dst_ref=got_s.at[p, N_SUB - 1 - o],
-            send_sem=ss_send.at[p, o - 1],
-            recv_sem=ss_recv.at[p, N_SUB - 1 - o],
-            device_id=sub_dev(o),
-        )
-
-    def sub_arrival(p, e):
-        return pltpu.make_async_remote_copy(
-            src_ref=pack.at[p, e],
-            dst_ref=got_s.at[p, e],
-            send_sem=ss_send.at[p, e],
-            recv_sem=ss_recv.at[p, e],
-            device_id=sub_dev(e + 1),
+            src_ref=pack.at[p, m - 1],
+            dst_ref=got_s.at[p, m - 1],
+            send_sem=ss_send.at[p, m - 1],
+            recv_sem=ss_recv.at[p, m - 1],
+            device_id=sub_dev(m),
         )
 
     def row_copy(j):
@@ -189,22 +185,24 @@
         )
 
     def send(p):
-        for j in (1, 3, 0, 2):
+        for j in (1, 3):
             dom_copy(p, j).start()
 
         if isinstance(p, int) and p == 0:
             for copy in small[2:]:
                 copy.wait()
-        order = (4, 3, 5, 2, 6, 1, 7)
+        order = FAR + NEAR
         for n, o in enumerate(order):
             for s in range(SS):
-                block = srow_m[lax.rem(b + o, N_SUB) * SS + s]
+                block = srow_m[jnp.bitwise_xor(b, o) * SS + s]
                 values = x3[p, block]
                 for k in range(DIMS):
                     pack[p, o - 1, k, pl.ds(s, 1), :] = values[k : k + 1]
             if n:
                 sub_copy(p, order[n - 1]).start()
         sub_copy(p, order[-1]).start()
+        for j in (0, 2):
+            dom_copy(p, j).start()
 
     xg3 = xg.reshape(ROWS_X, 8, TILE)
 
@@ -214,33 +212,37 @@
             xg[pl.ds(base * 8 + k, count, stride=8), :] = high
             xg[pl.ds(base * 8 + DIMS + k, count, stride=8), :] = values[k] - high
 
-    def multiply(pair, first, second, slot):
-        left = jnp.concatenate(
-            [xg3[first], xg3[second]],
-            axis=0,
-        ).astype(BF16)
+    def multiply(slot, one, two, first, second):
+        left = jnp.concatenate([xg3[first], xg3[second]], axis=0).astype(BF16)
         out = jnp.dot(
             jnp.concatenate([left, left], axis=1),
             jnp.concatenate(
-                [tb[pair, 0, 0 : 2 * TILE, :], tb[pair, 1, 0 : 2 * TILE, :]], axis=1
+                [tb[one, 0 : 2 * TILE, :], tb[two, 0 : 2 * TILE, :]], axis=1
             ),
             preferred_element_type=F32,
         )
-        prod[pl.ds(pl.multiple_of(slot * 16, 16), 8), :] = out[0:8, 0:TILE]
-        prod[pl.ds(pl.multiple_of(slot * 16 + 8, 8), 8), :] = out[8:16, TILE : 2 * TILE]
+        prod[slot * 16 : slot * 16 + 8, :] = out[0:8, 0:TILE]
+        prod[slot * 16 + 8 : slot * 16 + 16, :] = out[8:16, TILE : 2 * TILE]
 
     def run(first, count):
-        def body(i, carry):
-            pair = first + i
-            multiply(pair, idx[2 * pair], idx[2 * pair + 1], pair)
-            return carry
-
-        lax.fori_loop(0, count, body, 0, unroll=True)
+        for slot in range(first, first + count):
+            one = 2 * slot
+            multiply(slot, one, one + 1, idx[one], idx[one + 1])
+
+    def run_sub(first, last):
+        for t in range(first, last, 2):
+            multiply(
+                PAIR_S + t // 2,
+                2 * PAIR_S + tab_m[0, t],
+                2 * PAIR_S + tab_m[0, t + 1],
+                tab_m[1, t],
+                tab_m[1, t + 1],
+            )
 
     def taken(first, count, k):
         return (
-            prod[pl.ds(first * 16 + k, count, stride=8), :]
-            + prod[pl.ds(first * 16 + DIMS + k, count, stride=8), :]
+            prod[pl.ds(first * 8 + k, count, stride=8), :]
+            + prod[pl.ds(first * 8 + DIMS + k, count, stride=8), :]
         )
 
     def terms_of(first, count):
@@ -248,21 +250,15 @@
         for k in range(DIMS):
             value = taken(first, count, k)
             high = value.astype(BF16)
-            rest = value - high.astype(F32)
-            middle = rest.astype(BF16)
-            terms += [high, middle, (rest - middle.astype(F32)).astype(BF16)]
+            terms += [high, (value - high.astype(F32)).astype(BF16)]
         return jnp.concatenate(terms, axis=1)
 
     def combine(select, terms):
         out = jnp.dot(select[...], terms, preferred_element_type=F32)
         sums = []
         for k in range(DIMS):
-            at = 3 * k * TILE
-            sums.append(
-                out[:, at + 2 * TILE : at + 3 * TILE]
-                + out[:, at + TILE : at + 2 * TILE]
-                + out[:, at : at + TILE]
-            )
+            at = 2 * k * TILE
+            sums.append(out[:, at + TILE : at + 2 * TILE] + out[:, at : at + TILE])
         return sums
 
     small[1].wait()
@@ -282,8 +278,36 @@
     tile_ids = lax.broadcasted_iota(jnp.int32, (NB, LT), 1)
     hit = jnp.logical_and(lcol_v[...] == block_ids, tile_ids < live_m[0])
     sel_l[...] = jnp.where(hit, 1.0, 0.0).astype(BF16)
+    square = (IFS, IFS)
+    down = lax.broadcasted_iota(jnp.int32, square, 0)
+    across = lax.broadcasted_iota(jnp.int32, square, 1)
+
+    def stand(values):
+        return jnp.sum(
+            jnp.where(down == across, values.astype(F32), 0.0), axis=1, keepdims=True
+        )
+
+    slot = sslot_v[...]
+    apart = jnp.bitwise_xor(jnp.right_shift(slot, 3), b)
+    place = BASE_S + (apart - 1) * SS + jnp.bitwise_and(slot, SS - 1)
+    key = lax.broadcasted_iota(jnp.int32, (1, IFS), 1) + jnp.where(
+        apart >= 4, TILE, 0
+    )
+    keys = stand(key)
+    rank = jnp.sum(
+        jnp.where(key.astype(F32) < keys, 1.0, 0.0), axis=1, keepdims=True
+    )
+    chosen = jnp.where(rank == across.astype(F32), 1.0, 0.0)
+    tab_v[...] = jnp.zeros_like(tab_v)
+    ranges = (IFS, ROWS_X, NB)
+    for n, values in enumerate((down.astype(F32), stand(place), stand(scol_v[...]))):
+        line = jnp.sum(chosen * values, axis=0, keepdims=True).astype(jnp.int32)
+        line = jnp.clip(line, 0, ranges[n] - 1)
+        tab_v[n : n + 1, 0:IFS] = line
+    tabled = pltpu.make_async_copy(tab_v, tab_m, tab_sem)
+    tabled.start()
     sel_r[:, 0:IFS] = jnp.where(
-        scol_v[...] == lax.broadcasted_iota(jnp.int32, (NB, IFS), 0), 1.0, 0.0
+        line == lax.broadcasted_iota(jnp.int32, (NB, IFS), 0), 1.0, 0.0
     ).astype(BF16)
     sel_r[:, IFS : IFS + IFD] = jnp.where(
         dcol_v[...] == lax.broadcasted_iota(jnp.int32, (NB, IFD), 0), 1.0, 0.0
@@ -294,22 +318,15 @@
         idx[t] = lrow_m[t]
         return carry
 
-    def put_sub(t, carry):
-        slot = sslot_m[t]
-        place = jnp.bitwise_and(jnp.right_shift(slot, 3) - b - 1, N_SUB - 1)
-        idx[2 * PAIR_S + t] = BASE_S + place * SS + jnp.bitwise_and(slot, SS - 1)
-        return carry
-
     lax.fori_loop(0, LT, put_local, 0, unroll=8)
-    lax.fori_loop(0, IFS, put_sub, 0, unroll=8)
 
     def convert(i):
         for half in range(2):
             tile = land[2 * i + half]
             high = tile.astype(BF16)
             low = (tile - high.astype(F32)).astype(BF16)
-            tb[i, half, 0:TILE, :] = high
-            tb[i, half, TILE : 2 * TILE, :] = low
+            tb[2 * i + half, 0:TILE, :] = high
+            tb[2 * i + half, TILE : 2 * TILE, :] = low
 
     def arrive(first, count):
         def body(n, carry):
@@ -401,11 +418,11 @@
 
         lax.fori_loop(0, count - 1, body, 0, unroll=4)
 
-    def met(p, first, count, columns):
+    def met(p, first, count, table, line, start=0):
         total = None
         for t in range(count):
-            at = (2 * first + t) * 8
-            term = x3[p, columns[0, t]] * prod[at : at + 8, :]
+            at = (first + t) * 8
+            term = x3[p, table[line, start + t]] * prod[at : at + 8, :]
             total = term if total is None else total + term
         return total
 
@@ -421,28 +438,36 @@
                 row_copy(j).wait_recv()
             moved.start()
             arrive(PAIR_S, IFS // 2)
-        inner = combine(sel_l, terms_of(PAIR_L, LT))
+        inner = combine(sel_l, terms_of(2 * PAIR_L, LT))
         for k in range(DIMS):
             acc[k] = mass_v[...] * x_v[p, k] + inner[k]
         if last:
             early_rows()
             for k in range(DIMS):
                 x3[p, :, DIMS + k, :] = x_v[p, k]
-        for o in (7, 1, 2, 6, 3, 5, 4):
-            e = N_SUB - 1 - o
-            sub_arrival(p, e).wait_recv()
-            split(BASE_S + e * SS, SS, [got_s[p, e, k] for k in range(DIMS)])
-        run(PAIR_S, IFS // 2)
+        def take(ms):
+            for m in ms:
+                sub_copy(p, m).wait_recv()
+                split(
+                    BASE_S + (m - 1) * SS, SS, [got_s[p, m - 1, k] for k in range(DIMS)]
+                )
+
         if first:
-            arrive(PAIR_D, IFD // 2)
-            arrive(PAIR_P, NB // 2)
-        held[...] = terms_of(PAIR_S, IFS)
+            tabled.wait()
+        take(NEAR[::-1])
+        run_sub(0, NEAR_TILES)
+        held[...] = terms_of(2 * PAIR_S, NEAR_TILES)
         if last:
-            bent[...] = met(p, PAIR_S, IFS, scol_m)
+            bent[...] = met(p, 2 * PAIR_S, NEAR_TILES, tab_m, 2)
             for k in range(DIMS):
                 bent[k : k + 1, :] += jnp.sum(
                     acc[k] * x_v[p, k], axis=0, keepdims=True
                 )
+        if first:
+            arrive(PAIR_D, IFD // 2)
+            arrive(PAIR_P, NB // 2)
+        take(FAR)
+        run_sub(NEAR_TILES, IFS)
         if first:
             moved.wait()
             lax.fori_loop(0, IFD, put_dom, 0, unroll=True)
@@ -451,12 +476,23 @@
             split(BASE_D + j * NB, NB, [got_d[p, j, k] for k in range(DIMS)])
         run(PAIR_D, IFD // 2)
         if last:
-            whole = bent[...] + met(p, PAIR_D, IFD, dcol_m)
+            whole = bent[...] + met(
+                p, 2 * PAIR_S + NEAR_TILES, IFS - NEAR_TILES, tab_m, 2, NEAR_TILES
+            )
+            whole = whole + met(p, 2 * PAIR_D, IFD, dcol_m, 0)
             to_row(1, whole[0:DIMS] + whole[DIMS : 2 * DIMS])
             for m in sorted(range(1, count), key=lambda m: -hops(m)):
                 row_to(1, m).start()
         outer = combine(
-            sel_r, jnp.concatenate([held[...], terms_of(PAIR_D, IFD)], axis=0)
+            sel_r,
+            jnp.concatenate(
+                [
+                    held[...],
+                    terms_of(2 * PAIR_S + NEAR_TILES, IFS - NEAR_TILES + IFD),
+                ],
+                axis=0,
+            ),
+
         )
         for k in range(DIMS):
             value = acc[k] + outer[k]
@@ -469,9 +505,10 @@
         if not last:
             split(0, NB, [q_v[p, k] for k in range(DIMS)])
             for i in range(NB // 2):
-                multiply(PAIR_P + i, 2 * i, 2 * i + 1, PAIR_P + i)
+                one = 2 * (PAIR_P + i)
+                multiply(PAIR_P + i, one, one + 1, 2 * i, 2 * i + 1)
             for k in range(DIMS):
-                value = taken(PAIR_P, NB, k)
+                value = taken(2 * PAIR_P, NB, k)
                 x_v[p + 1, k] = value
                 x3[p + 1, :, k, :] = value
 
@@ -600,7 +637,7 @@
             pltpu.VMEM((3, DIMS, NB, TILE), F32),
             pltpu.VMEM((NB, TILE), F32),
             pltpu.VMEM((2 * PAIRS, TILE, TILE), F32),
-            pltpu.VMEM((PAIRS, 2, 2 * TILE + 16, TILE), BF16),
+            pltpu.VMEM((2 * PAIRS, 2 * TILE + 16, TILE), BF16),
             pltpu.VMEM((ROWS_X * 8, TILE), F32),
             pltpu.VMEM((PAIRS * 16, TILE), F32),
             pltpu.VMEM((DIMS, NB, TILE), F32),
@@ -609,10 +646,12 @@
             pltpu.VMEM((PHASES, N_SUB - 1, DIMS, SS, TILE), F32),
             pltpu.VMEM((NB, LT), BF16),
             pltpu.VMEM((NB, IFS + IFD), BF16),
-            pltpu.VMEM((IFS, 9 * TILE), BF16),
+            pltpu.VMEM((NEAR_TILES, 2 * DIMS * TILE), BF16),
             pltpu.VMEM((1, LT), jnp.int32),
             pltpu.VMEM((1, IFS), jnp.int32),
             pltpu.VMEM((1, IFD), jnp.int32),
+            pltpu.VMEM((1, IFS), jnp.int32),
+            pltpu.VMEM((8, TILE), jnp.int32),
             pltpu.VMEM((4, TILE), jnp.int32),
             pltpu.VMEM((BITS, 4, TILE), jnp.int32),
             pltpu.VMEM((24, TILE), F32),
@@ -622,18 +661,18 @@
             pltpu.VMEM((2, N_DOM * N_SUB, TILE), F32),
             pltpu.SMEM((LT,), jnp.int32),
             pltpu.SMEM((1,), jnp.int32),
-            pltpu.SMEM((IFS,), jnp.int32),
             pltpu.SMEM((N_SUB * SS,), jnp.int32),
             pltpu.SMEM((IFD,), jnp.int32),
             pltpu.SMEM((BITS, 4, TILE), jnp.int32),
-            pltpu.SMEM((1, IFS), jnp.int32),
             pltpu.SMEM((1, IFD), jnp.int32),
+            pltpu.SMEM((8, TILE), jnp.int32),
             pltpu.SMEM((2 * PAIR_P,), jnp.int32),
             pltpu.SMEM((3, IFD), jnp.int32),
-            dma((13,)),
+            dma((12,)),
             dma((2 * PAIRS // GROUP,)),
             dma((BITS,)),
             dma((BITS,)),
+            dma,
             dma,
             dma((PHASES, BITS)),
             dma((PHASES, BITS)),
@@ -658,7 +697,7 @@
         dom_rows.reshape(4, TILE),
         sub_tiles,
         sub_cols.reshape(1, IFS),
-        sub_slots,
+        sub_slots.reshape(1, IFS),
         sub_rows,
         precond,
     )

time: 38.8 us -> 38.3 us (0.987)
  Pallas kernels: 36.6 us -> 36.2 us
    pallas_call x1, Pallas kernels: 36.6 us -> 36.2 us  [on_device(): pl.pallas_call(kernel, out_shape=(pltpu.VMEM((DIMS, NB, TILE), F32),) * 2...]
where the time goes in v4:
time: 38.3 us; the launch traced here: 38.2 us
  Pallas kernels  36.2 us (95%)
  between operations  1.29 us (3%)
  local copies, waits for them, and re-layouts  0.72 us (2%)
    pallas_call x1, Pallas kernels, on_device(): pl.pallas_call(kernel, out_shape=(pltpu.VMEM((DIMS, NB, TILE), F32),) * 2...  36.2 us

profile of v4, /device:TPU:1, one launch (start us, length us, event | category | flops | bytes accessed | tf_op | source)
XLA Modules:
  0.0 38.2 jit_solution(9704288081890841327)
XLA Ops:
  1.3 36.2 %shard_map.158 = (f32[3,32,128]{2,1,0:T(8,128)S(1)}, f32[3,32,128]{2,1,0:T(8,128)S(1)}) custom-call(f32[3,4096]{1,0:T(4,128)} %pos_h.1, f32[32,128]{1,0:T(8,128)} %bitcast.14, f32[64,128,128]{2,1,0:T(8,128)} %lt_h.1, s32[64]{0:T(128)} %lrow_h.1, s32[1,64]{1,0:T(1,128)} %bitcast.16, s32[1]{0:T(128)S(6)} %copy.21.live_h, f32[32,128,128]{2,1,0:T(8,128)} %dt_h.1, ...), custom_call_target="tpu_custom_call" | custom-call | tf_op jit(solution)/shard_map/pallas_call | solution.py:627
  37.4 0.7 %copy_bitcast_fusion = (f32[3,4096]{1,0:T(4,128)}, f32[3,4096]{1,0:T(4,128)}) fusion(f32[1,3,32,128]{3,2,1,0:T(8,128)S(1)} %bitcast.13, f32[1,3,32,128]{3,2,1,0:T(8,128)S(1)} %bitcast.12), kind=kLoop, calls=%fused_computation | loop fusion | bytes 196608 | tf_op jit(solution)/shard_map/reshape | solution.py:704

commit v5 on v4

--- a/solution.py
+++ b/solution.py
@@ -426,6 +426,12 @@
             total = term if total is None else total + term
         return total
 
+    def drain(p):
+        for j in range(BITS):
+            dom_copy(p, j).wait_send()
+        for m in range(1, N_SUB):
+            sub_copy(p, m).wait_send()
+
     def phase(p, first, last):
         if first:
             arrive(PAIR_L, LT // 2)
@@ -438,6 +444,11 @@
                 row_copy(j).wait_recv()
             moved.start()
             arrive(PAIR_S, IFS // 2)
+        if first:
+            for j in range(BITS):
+                row_copy(j).wait_send()
+        else:
+            drain(p - 1)
         inner = combine(sel_l, terms_of(2 * PAIR_L, LT))
         for k in range(DIMS):
             acc[k] = mass_v[...] * x_v[p, k] + inner[k]
@@ -471,7 +482,7 @@
         if first:
             moved.wait()
             lax.fori_loop(0, IFD, put_dom, 0, unroll=True)
-        for j in (0, 2, 1, 3):
+        for j in (1, 3, 0, 2):
             dom_copy(p, j).wait_recv()
             split(BASE_D + j * NB, NB, [got_d[p, j, k] for k in range(DIMS)])
         run(PAIR_D, IFD // 2)
@@ -520,6 +531,8 @@
     lax.fori_loop(1, PHASES - 1, later, 0)
     phase(PHASES - 1, False, True)
 
+    drain(PHASES - 1)
+    row_all(0).wait_send()
     row_all(0).wait_recv()
     wide = jnp.broadcast_to(jnp.sum(rows[0], axis=0, keepdims=True), (8, TILE))
     values = [wide] + [pltpu.roll(wide, TILE - DIMS * n, 1) for n in range(1, 6)]
@@ -594,15 +607,7 @@
         sol_o[k] = last_v[0, k] + scale * last_v[1, k]
         res_o[k] = last_v[2, k] - scale * last_v[3, k]
 
-    for which in range(2):
-        row_all(which).wait_send()
-    for j in range(BITS):
-        row_copy(j).wait_send()
-    for p in range(PHASES):
-        for j in range(BITS):
-            dom_copy(p, j).wait_send()
-        for o in range(1, N_SUB):
-            sub_copy(p, o).wait_send()
+    row_all(1).wait_send()
 
 
 def on_device(
@@ -632,14 +637,14 @@
         scratch_shapes=[
             pltpu.VMEM((DIMS, NB * TILE), F32),
             pltpu.VMEM((PHASES, DIMS, NB, TILE), F32),
-            pltpu.VMEM((PHASES, NB, 8, TILE), F32),
+            pltpu.VMEM((PHASES + 1, NB, 8, TILE), F32),
             pltpu.VMEM((3, DIMS, NB, TILE), F32),
             pltpu.VMEM((3, DIMS, NB, TILE), F32),
             pltpu.VMEM((NB, TILE), F32),
             pltpu.VMEM((2 * PAIRS, TILE, TILE), F32),
             pltpu.VMEM((2 * PAIRS, 2 * TILE + 16, TILE), BF16),
             pltpu.VMEM((ROWS_X * 8, TILE), F32),
-            pltpu.VMEM((PAIRS * 16, TILE), F32),
+            pltpu.VMEM((PAIRS * 16 + 8, TILE), F32),
             pltpu.VMEM((DIMS, NB, TILE), F32),
             pltpu.VMEM((PHASES, BITS, DIMS, NB, TILE), F32),
             pltpu.VMEM((PHASES, N_SUB - 1, DIMS, SS, TILE), F32),

time: 38.3 us -> 38.2 us (level)
  no operation moved by 1% of the time
where the time goes in v5:
time: 38.2 us; the launch traced here: 38.1 us
  Pallas kernels  36.1 us (95%)
  between operations  1.29 us (3%)
  local copies, waits for them, and re-layouts  0.72 us (2%)
    pallas_call x1, Pallas kernels, on_device(): pl.pallas_call(kernel, out_shape=(pltpu.VMEM((DIMS, NB, TILE), F32),) * 2...  36.1 us

profile of v5, /device:TPU:1, one launch (start us, length us, event | category | flops | bytes accessed | tf_op | source)
XLA Modules:
  0.0 38.1 jit_solution(4186073978020734472)
XLA Ops:
  1.3 36.1 %shard_map.158 = (f32[3,32,128]{2,1,0:T(8,128)S(1)}, f32[3,32,128]{2,1,0:T(8,128)S(1)}) custom-call(f32[3,4096]{1,0:T(4,128)} %pos_h.1, f32[32,128]{1,0:T(8,128)} %bitcast.14, f32[64,128,128]{2,1,0:T(8,128)} %lt_h.1, s32[64]{0:T(128)} %lrow_h.1, s32[1,64]{1,0:T(1,128)} %bitcast.16, s32[1]{0:T(128)S(6)} %copy.21.live_h, f32[32,128,128]{2,1,0:T(8,128)} %dt_h.1, ...), custom_call_target="tpu_custom_call" | custom-call | tf_op jit(solution)/shard_map/pallas_call | solution.py:632
  37.4 0.7 %copy_bitcast_fusion = (f32[3,4096]{1,0:T(4,128)}, f32[3,4096]{1,0:T(4,128)}) fusion(f32[1,3,32,128]{3,2,1,0:T(8,128)S(1)} %bitcast.13, f32[1,3,32,128]{3,2,1,0:T(8,128)S(1)} %bitcast.12), kind=kLoop, calls=%fused_computation | loop fusion | bytes 196608 | tf_op jit(solution)/shard_map/reshape | solution.py:709
